TPU v7x, 32 devices: a whole 2x2x4 slice. The times are simulated.
32 devices in a mesh: group: 4 (over y, core), peer: 8 (over z, x).
Axes of the slice: x: 2, y: 2, z: 4, core: 2. Of those that a mesh axis runs over, the one named last changes fastest.
Arguments:
- states: float32 [41, 1048576], P(None, ('group', 'peer')), may hold values from -6 to 6
- block_part: int32 [8192], P(('group', 'peer')), may hold values from 0 to 31, as said below
- tile_perm: int32 [8192, 128], P(('group', 'peer')), may hold values from 0 to 127, each once within a row
- half_volt: float32 [40], replicated, may hold values from -4 to 4
- steepness: float32 [40], replicated, may hold values from 0.5 to 4
- gate_rate: float32 [40], replicated, may hold values from 0.1 to 1
- conductance: float32 [40], replicated, may hold values from 0.005 to 0.08
- reversal: float32 [40], replicated, may hold values from -6 to 6
Outputs:
- regrouped: float32 [41, 1048576], P(None, ('group', 'peer'))
Inputs may be any that keep to these rules, and one draw needn't show every extreme that they name: `block_part`: every partition holds exactly 256 blocks. Within each slab of 256 consecutive global blocks no partition holds more than 16 blocks; every slab has exactly 16 blocks of some partition, and every partition has exactly 16 blocks in some slab.
All inputs are finite; a program needn't handle non-finite values.
Results may differ from a plain program's by a relative error of at most 0.0001.
Values sent between devices are 32-bit elements; how exact they have to be, the bound alone decides.
A program may use at most 192 MiB of HBM per device.

v0:
```python
import functools
import jax
import jax.numpy as jnp
import numpy as np
from jax import lax
from jax.experimental import pallas as pl
from jax.experimental.pallas import tpu as pltpu
from jax.sharding import PartitionSpec as P

time_step = 0.25
LANES = 128
ROWS = 8
MESH_ID = pl.DeviceIdType.MESH
VMEM_LIMIT = 67043328
SLOTS = (184, 208, 216, 200, 184)
ORDERS = ((2, 1, 4, 0, 3), (1, 2, 4, 0, 3), (0, 4, 3, 2, 1), (0, 4, 3, 1, 2))


def submasks(bits):
    masks = [0]
    for bit in bits:
        masks = masks + [m | (1 << bit) for m in masks]
    return sorted(masks)


def stage_pairs(order, j):
    before, after = order[:j], order[j + 1 :]
    here = 1 << order[j]
    return [(a, b | here) for a in submasks(before) for b in submasks(after)]


def flip(d, mask):
    out = d
    bit = 0
    while (1 << bit) <= mask:
        if mask & (1 << bit):
            out = out + (1 - 2 * ((d // (1 << bit)) % 2)) * (1 << bit)
        bit += 1
    return out


def my_index(peers):
    return lax.axis_index("group") * peers + lax.axis_index("peer")


def counts_kernel(devices, peers, x_ref, out_ref, send_sem, recv_sem, local_sem):
    d = my_index(peers)
    barrier = pltpu.get_barrier_semaphore()
    for k in range(1, devices):
        to = (d + k) % devices
        pl.semaphore_signal(
            barrier, inc=1, device_id=(to // peers, to % peers), device_id_type=MESH_ID
        )
    pl.semaphore_wait(barrier, devices - 1)
    own = pltpu.make_async_copy(x_ref.at[0], out_ref.at[d], local_sem)
    own.start()
    for k in range(1, devices):
        to = (d + k) % devices
        pltpu.make_async_remote_copy(
            src_ref=x_ref.at[0], dst_ref=out_ref.at[d],
            send_sem=send_sem.at[k], recv_sem=recv_sem.at[k],
            device_id=(to // peers, to % peers), device_id_type=MESH_ID,
        ).start()
    own.wait()
    for k in range(1, devices):
        src = (d + devices - k) % devices
        pltpu.make_async_remote_copy(
            src_ref=x_ref.at[0], dst_ref=out_ref.at[src],
            send_sem=send_sem.at[k], recv_sem=recv_sem.at[k],
            device_id=(src // peers, src % peers), device_id_type=MESH_ID,
        ).wait()


def gather_counts(row, devices, peers):
    return pl.pallas_call(
        functools.partial(counts_kernel, devices, peers),
        out_shape=jax.ShapeDtypeStruct((devices, 1, LANES), jnp.int32),
        in_specs=[pl.BlockSpec(memory_space=pltpu.VMEM)],
        out_specs=pl.BlockSpec(memory_space=pltpu.VMEM),
        scratch_shapes=[
            pltpu.SemaphoreType.DMA((devices,)),
            pltpu.SemaphoreType.DMA((devices,)),
            pltpu.SemaphoreType.DMA,
        ],
        compiler_params=pltpu.CompilerParams(collective_id=0, has_side_effects=True),
    )(row)


def table_kernel(
    devices, peers, own_blocks, slots, c_ref, part_ref, tables_ref, final_ref, earlier
):
    d = my_index(peers)
    pool_size = own_blocks + sum(slots)
    run = jnp.int32(0)
    for s in range(devices):
        earlier[s] = run
        run = run + c_ref[s, 0, d]
    shape = (ROWS, LANES)
    flat = lax.broadcasted_iota(jnp.int32, shape, 0) * LANES + lax.broadcasted_iota(
        jnp.int32, shape, 1
    )
    part = part_ref[...]
    sources = lax.broadcasted_iota(jnp.int32, (devices, own_blocks), 0)
    onehot = part == sources
    onehot_f = onehot.astype(jnp.float32)
    upper = (
        lax.broadcasted_iota(jnp.int32, (own_blocks, own_blocks), 0)
        < lax.broadcasted_iota(jnp.int32, (own_blocks, own_blocks), 1)
    ).astype(jnp.float32)
    rank = jnp.dot(onehot_f, upper, preferred_element_type=jnp.float32).astype(jnp.int32)
    near = lax.broadcasted_iota(jnp.int32, (devices, LANES), 0)
    final_ref[...] = jnp.zeros_like(final_ref)
    for o, order in enumerate(ORDERS):
        pos = {(0, m): earlier[flip(d, m)] for m in range(devices)}
        for j, bit in enumerate(order):
            pairs = stage_pairs(order, j)
            table = flat
            start = jnp.int32(0)
            shift = jnp.int32(0)
            for a, b in pairs:
                now = pos[(a, b)] - start
                table = table + jnp.where(flat >= start, now - shift, 0)
                shift = now
                start = start + c_ref[flip(d, b), 0, flip(d, a)]
            table = jnp.where(flat < start, table, 0)
            row = (o * len(order) + j) * 2
            tables_ref[row : row + 2, :] = table[0:2]
            fresh = {
                k: v for k, v in pos.items() if not (k[1] >> bit) & 1
            }
            partner = flip(d, 1 << bit)
            start = jnp.int32(own_blocks + sum(slots[:j]))
            for a, b in pairs:
                fresh[(a | (1 << bit), b ^ (1 << bit))] = start
                start = start + c_ref[flip(partner, b), 0, flip(partner, a)]
            pos = fresh
        base = jnp.zeros((devices, LANES), jnp.int32)
        for a in range(devices):
            base = jnp.where(near == flip(d, a), pos[(a, 0)], base)
        whole = jnp.sum(jnp.where(onehot, base[:, 0:1] + rank, 0), axis=0, keepdims=True)
        whole = jnp.clip(whole, 0, pool_size - 1)
        final_ref[o : o + 1, :] = whole


def make_tables(counts, part, devices, peers, own_blocks, slots):
    return pl.pallas_call(
        functools.partial(table_kernel, devices, peers, own_blocks, slots),
        out_shape=(
            jax.ShapeDtypeStruct((2 * len(ORDERS) * len(slots), LANES), jnp.int32),
            jax.ShapeDtypeStruct((8, own_blocks), jnp.int32),
        ),
        in_specs=[
            pl.BlockSpec(memory_space=pltpu.SMEM),
            pl.BlockSpec(memory_space=pltpu.VMEM),
        ],
        out_specs=(
            pl.BlockSpec(memory_space=pltpu.VMEM),
            pl.BlockSpec(memory_space=pltpu.VMEM),
        ),
        scratch_shapes=[pltpu.SMEM((devices,), jnp.int32)],
    )(counts, part)


def messages_fit(counts, devices):
    ids = np.arange(devices)
    apart = ids[:, None] ^ ids[None, :]
    to_rows, from_rows, room = [], [], []
    for order in ORDERS:
        for j, bit in enumerate(order):
            before = sum(1 << b for b in order[:j])
            after = sum(1 << b for b in order[j + 1 :])
            here = 1 << bit
            to_rows.append(((apart & before) == 0) & ((apart & here) != 0))
            from_rows.append((apart & (here | after)) == 0)
            room.append(np.full((devices,), SLOTS[j]))
    to_rows = jnp.asarray(np.concatenate(to_rows), jnp.bfloat16)
    from_rows = jnp.asarray(np.concatenate(from_rows), jnp.float32)
    part = jnp.dot(
        to_rows, counts.astype(jnp.bfloat16), preferred_element_type=jnp.float32
    )
    room = jnp.asarray(np.concatenate(room), jnp.float32)
    return jnp.max(jnp.sum(part * from_rows, axis=1) - room) <= 0.0


EVENTS = (
    (1, 0), (0, 0), (3, 0), (4, 0), (5, 0), (3, 1), (5, 1), (0, 1), (1, 1), (4, 1),
    (3, 2), (5, 2), (4, 2), (2, 0), (3, 3), (0, 2), (1, 2), (4, 3), (0, 3), (1, 3),
    (0, 4), (1, 4), (2, 1), (3, 4), (5, 3), (0, 5), (1, 5), (4, 4), (2, 2), (5, 4),
    (2, 3), (2, 4), (2, 5), (3, 5), (5, 5), (4, 5),
)
CHUNK_ORDER = (0, 1, 1, 2, 3, 2)
BUFFERS = {2: (0, 1), 1: (2, 3), 0: (4, 5), 4: (6,), 3: (7,)}


def exchange_kernel(
    peers, own_blocks, slots, unroll,
    tables, finals, params, states, out, out_row,
    pool, pool_row, landed, landed_row, packed, packed_row, ready, ready_row,
    send_sem, recv_sem, out_sem,
):
    d = my_index(peers)
    barrier = pltpu.get_barrier_semaphore()
    bits = sorted(ORDERS[0])
    for bit in bits:
        to = flip(d, 1 << bit)
        pl.semaphore_signal(
            barrier, inc=1, device_id=(to // peers, to % peers), device_id_type=MESH_ID
        )

    tiles = pool.shape[0]

    def advance_block(b):
        cols = pl.ds(pl.multiple_of(b * LANES, LANES), LANES)
        top = states[0:ROWS, cols]
        voltage = top[0:1, :]
        spread = jnp.broadcast_to(voltage, (ROWS, LANES))
        slow = -(1.0 + jax.nn.sigmoid(spread))

        def gates(vals, base, count):
            half, steep, rate, cond, rev = (
                params[k, base : base + count, :] for k in range(5)
            )
            v = spread[0:count]
            steady = jax.nn.sigmoid((v - half) * steep)
            damping = jnp.exp(rate * slow[0:count])
            new = steady + (vals - steady) * damping
            return new, cond * new * (v - rev)

        total = jnp.zeros((ROWS, LANES), jnp.float32)
        for t in range(1, tiles):
            new, term = gates(states[t * ROWS : (t + 1) * ROWS, cols], t * ROWS, ROWS)
            pool[t, b] = new
            total = total + term
        last = tiles * ROWS
        new_row, term_row = gates(states[last : last + 1, cols], last, 1)
        pool_row[pl.ds(b, 1), :] = new_row
        new, term = gates(top, 0, ROWS)
        total = total + term
        current = jnp.sum(total, axis=0, keepdims=True) + term_row
        moved = voltage - time_step * current
        first = lax.broadcasted_iota(jnp.int32, (ROWS, LANES), 0) == 0
        pool[0, b] = jnp.where(first, jnp.broadcast_to(moved, (ROWS, LANES)), new)

    def advance_loop(i, _):
        for u in range(4):
            advance_block(i * 4 + u)
        return 0

    lax.fori_loop(0, own_blocks // 4, advance_loop, 0)
    pl.semaphore_wait(barrier, len(bits))

    stages = len(bits)
    used = {}
    copies = {}
    outs = []
    turn = {bit: 0 for bit in bits}

    def arrive(c, j):
        copies[(c, j)].wait_recv()
        begin = sum(slots[:j])
        base = own_blocks + begin

        def move(i, _):
            for u in range(unroll):
                k = i * unroll + u
                if c < tiles:
                    pool[c, base + k] = landed[c, begin + k]
            return 0

        if c < tiles:
            lax.fori_loop(0, slots[j] // unroll, move, 0)
        else:
            pool_row[base : base + slots[j], :] = landed_row[begin : begin + slots[j], :]

    for c, j in EVENTS:
        order = ORDERS[CHUNK_ORDER[c]]
        if j > 0:
            arrive(c, j - 1)
        if j < stages:
            bit = order[j]
            if c < tiles:
                names = BUFFERS[bit]
                buf = names[turn[bit] % len(names)]
                turn[bit] += 1
                if buf in used:
                    copies[used[buf]].wait_send()
                used[buf] = (c, j)
            begin, room = sum(slots[:j]), slots[j]
            row = (CHUNK_ORDER[c] * stages + j) * 2 * LANES

            def pack(i, _):
                for u in range(unroll):
                    k = i * unroll + u
                    at = tables[row + k]
                    if c < tiles:
                        packed[buf, k] = pool[c, at]
                    else:
                        packed_row[pl.ds(begin + k, 1), :] = pool_row[pl.ds(at, 1), :]
                return 0

            lax.fori_loop(0, room // unroll, pack, 0)
            to = flip(d, 1 << bit)
            copy = pltpu.make_async_remote_copy(
                src_ref=packed.at[buf, pl.ds(0, room)]
                if c < tiles
                else packed_row.at[pl.ds(begin, room)],
                dst_ref=landed.at[c, pl.ds(begin, room)]
                if c < tiles
                else landed_row.at[pl.ds(begin, room)],
                send_sem=send_sem.at[c, j],
                recv_sem=recv_sem.at[c, j],
                device_id=(to // peers, to % peers),
                device_id_type=MESH_ID,
            )
            copy.start()
            copies[(c, j)] = copy
        else:
            if c < tiles and outs:
                outs.pop().wait()
            first = CHUNK_ORDER[c] * own_blocks

            def pick(i, _):
                for u in range(unroll):
                    k = i * unroll + u
                    at = finals[first + k]
                    if c < tiles:
                        ready[k] = pool[c, at]
                    else:
                        ready_row[pl.ds(k, 1), :] = pool_row[pl.ds(at, 1), :]
                return 0

            lax.fori_loop(0, own_blocks // unroll, pick, 0)
            if c < tiles:
                copy = pltpu.make_async_copy(ready, out.at[c], out_sem.at[0])
                copy.start()
                outs.append(copy)
            else:
                row_copy = pltpu.make_async_copy(ready_row, out_row, out_sem.at[1])
                row_copy.start()
    row_copy.wait()
    for copy in outs:
        copy.wait()
    last_use = set(used.values()) | {(tiles, j) for j in range(stages)}
    for key in sorted(last_use):
        copies[key].wait_send()


def exchange(tables, finals, params, states, peers, own_blocks, slots):
    tiles = states.shape[0] // ROWS
    stages = len(ORDERS[0])
    size = own_blocks + sum(slots)
    f32 = jnp.float32
    return pl.pallas_call(
        functools.partial(exchange_kernel, peers, own_blocks, slots, 8),
        out_shape=(
            jax.ShapeDtypeStruct((tiles, own_blocks, ROWS, LANES), f32),
            jax.ShapeDtypeStruct((own_blocks, LANES), f32),
        ),
        in_specs=[
            pl.BlockSpec(memory_space=pltpu.SMEM),
            pl.BlockSpec(memory_space=pltpu.SMEM),
            pl.BlockSpec(memory_space=pltpu.VMEM),
            pl.BlockSpec(memory_space=pltpu.VMEM),
        ],
        out_specs=(
            pl.BlockSpec(memory_space=pl.ANY),
            pl.BlockSpec(memory_space=pl.ANY),
        ),
        scratch_shapes=[
            pltpu.VMEM((tiles, size, ROWS, LANES), f32),
            pltpu.VMEM((size, LANES), f32),
            pltpu.VMEM((tiles, sum(slots), ROWS, LANES), f32),
            pltpu.VMEM((sum(slots), LANES), f32),
            pltpu.VMEM((1 + max(max(b) for b in BUFFERS.values()), max(slots), ROWS, LANES), f32),
            pltpu.VMEM((sum(slots), LANES), f32),
            pltpu.VMEM((own_blocks, ROWS, LANES), f32),
            pltpu.VMEM((own_blocks, LANES), f32),
            pltpu.SemaphoreType.DMA((tiles + 1, stages)),
            pltpu.SemaphoreType.DMA((tiles + 1, stages)),
            pltpu.SemaphoreType.DMA((2,)),
        ],
        compiler_params=pltpu.CompilerParams(
            collective_id=1, has_side_effects=True, vmem_limit_bytes=VMEM_LIMIT
        ),
    )(tables, finals, params, states)


def place_kernel(tiles, blocks, got, got_row, perm, out):
    for group in range(blocks // ROWS):
        rows = slice(group * ROWS, (group + 1) * ROWS)
        turned = jnp.take_along_axis(
            got_row[rows, :], perm[rows, :], axis=1, mode="promise_in_bounds"
        )
        for u in range(ROWS):
            b = group * ROWS + u
            cols = slice(b * LANES, (b + 1) * LANES)
            where = jnp.broadcast_to(perm[b : b + 1, :], (ROWS, LANES))
            for t in range(tiles):
                out[t * ROWS : (t + 1) * ROWS, cols] = jnp.take_along_axis(
                    got[t, b], where, axis=1, mode="promise_in_bounds"
                )
            out[tiles * ROWS : tiles * ROWS + 1, cols] = turned[u : u + 1, :]


def place(got, got_row, perm, width, own_blocks):
    tiles = got.shape[0]
    step = 32
    return pl.pallas_call(
        functools.partial(place_kernel, tiles, step),
        grid=(own_blocks // step,),
        out_shape=jax.ShapeDtypeStruct((width, own_blocks * LANES), jnp.float32),
        in_specs=[
            pl.BlockSpec((tiles, step, ROWS, LANES), lambda i: (0, i, 0, 0)),
            pl.BlockSpec((step, LANES), lambda i: (i, 0)),
            pl.BlockSpec((step, LANES), lambda i: (i, 0)),
        ],
        out_specs=pl.BlockSpec((width, step * LANES), lambda i: (0, i)),
    )(got, got_row, perm)


def advance(state_rows, half_volt, steepness, gate_rate, conductance, reversal):
    voltage = state_rows[0:1]
    gate_vals = state_rows[1:]
    steady = jax.nn.sigmoid((voltage - half_volt[:, None]) * steepness[:, None])
    damping = jnp.exp(-gate_rate[:, None] * (1.0 + jax.nn.sigmoid(voltage)))
    gate_vals = steady + (gate_vals - steady) * damping
    current = jnp.sum(
        conductance[:, None] * gate_vals * (voltage - reversal[:, None]), axis=0, keepdims=True
    )
    voltage = voltage - time_step * current
    return jnp.concatenate([voltage, gate_vals], axis=0)


def general(counts_all, devices, states, block_part, tile_perm, *gate_params):
    d = lax.axis_index(("group", "peer"))
    local_blocks = block_part.shape[0]
    tile_width = tile_perm.shape[1]
    width = states.shape[0]
    capacity = 2 * local_blocks // devices
    partitions = jnp.arange(devices, dtype=jnp.int32)
    onehot = (block_part[:, None] == partitions[None, :]).astype(jnp.int32)
    before = (partitions < d).astype(jnp.int32)
    earlier = jnp.sum(counts_all * before[:, None], axis=0, dtype=jnp.int32)
    rank_in = jnp.sum(
        (jnp.cumsum(onehot, axis=0, dtype=jnp.int32) - onehot) * onehot, axis=1, dtype=jnp.int32
    )
    local_index = jnp.sum(onehot * earlier[None, :], axis=1, dtype=jnp.int32) + rank_in
    slot_index = block_part * capacity + rank_in
    requests = jnp.full((devices * capacity,), -1, jnp.int32).at[slot_index].set(local_index)
    requests = requests.reshape(devices, capacity)
    advanced = advance(states, *gate_params)
    advanced = advanced.reshape(width, local_blocks, tile_width)
    wanted = lax.all_to_all(requests, ("group", "peer"), split_axis=0, concat_axis=0, tiled=True)
    picked = jnp.maximum(wanted, 0).reshape(-1)
    served = jnp.take(advanced, picked, axis=1)
    arrived = lax.all_to_all(
        served.reshape(width, wanted.shape[0], wanted.shape[1], tile_width),
        ("group", "peer"), split_axis=1, concat_axis=1, tiled=True,
    )
    flat_cols = (slot_index[:, None] * tile_width + tile_perm).reshape(-1)
    return jnp.take(arrived.reshape(width, devices * capacity * tile_width), flat_cols, axis=1)


def on_device(devices, peers, states, block_part, tile_perm, *gate_params):
    own_blocks = block_part.shape[0]
    width = states.shape[0]
    partitions = jnp.arange(LANES, dtype=jnp.int32)
    counts = jnp.sum(
        (block_part[:, None] == partitions[None, :]).astype(jnp.int32), axis=0, dtype=jnp.int32
    )
    if devices != 1 << len(ORDERS[0]) or width % ROWS != 1:
        gathered = lax.all_gather(counts[:devices], ("group", "peer"))
        return general(gathered, devices, states, block_part, tile_perm, *gate_params)
    gathered = gather_counts(counts.reshape(1, 1, LANES), devices, peers)
    matrix = gathered[:, 0, :devices]
    fits = messages_fit(matrix, devices)
    tables, finals = make_tables(
        gathered, block_part.reshape(1, own_blocks), devices, peers, own_blocks, SLOTS
    )
    table_list = tables.reshape(-1)
    final_list = finals[0 : len(ORDERS)].reshape(-1)
    padded = jnp.stack([jnp.pad(p, (1, 0)) for p in gate_params])
    params = jnp.broadcast_to(padded[:, :, None], padded.shape + (LANES,))

    def fast():
        got, got_row = exchange(
            table_list, final_list, params, states, peers, own_blocks, SLOTS
        )
        return place(got, got_row, tile_perm, width, own_blocks)

    def slow():
        return general(matrix, devices, states, block_part, tile_perm, *gate_params)

    return lax.cond(fits, fast, slow)


def solution(mesh):
    both = P(("group", "peer"))
    return jax.shard_map(
        functools.partial(on_device, mesh.devices.size, mesh.shape["peer"]),
        mesh=mesh,
        in_specs=(P(None, ("group", "peer")), both, P(("group", "peer"), None)) + (P(),) * 5,
        out_specs=P(None, ("group", "peer")),
        check_vma=False,
    )
```

profile of v0, /device:TPU:9, one launch (start us, length us, event | category | flops | bytes accessed | tf_op | source)
XLA Modules:
  0.0 229.4 jit_solution(11040844380587666568)
XLA Ops:
  0.0 0.7 pad_bitcast_fusion.4
  0.7 1.3 convert_reduce_fusion
  2.0 0.7 pad_bitcast_fusion.2
  2.8 0.7 pad_bitcast_fusion
  3.6 9.0 %shard_map.111.c_ref = s32[32,1,128]{2,1,0:T(1,128)S(1)} custom-call(s32[1,1,128]{2,1,0:T(1,128)} %bitcast.77), custom_call_target="tpu_custom_call" | custom-call | tf_op jit(solution)/shard_map/pallas_call | solution.py:75
  12.5 1.2 fusion.6
  13.7 1.3 add_reduce_fusion
  15.7 2.9 %shard_map.112 = (s32[40,128]{1,0:T(8,128)}, s32[8,256]{1,0:T(8,128)S(1)}) custom-call(s32[32,1,128]{2,1,0:T(1,128)S(1)} %shard_map.111.c_ref, s32[1,256]{1,0:T(1,128)} %bitcast.75), custom_call_target="tpu_custom_call" | custom-call | tf_op jit(solution)/shard_map/pallas_call | solution.py:146
  18.6 210.8 %conditional.1 = (f32[41,32768]{1,0:T(8,128)}) conditional(s32[]{:T(128)} %convert_element_type.31, (s32[256]{0:T(256)}, s32[256,128]{1,0:T(8,128)}, s32[32,32]{1,0:T(8,128)S(1)}, f32[41,32768]{1,0:T(8,128)}, f32[40]{0:T(128)}, /*index=5*/f32[40]{0:T(128)}, f32[40]{0:T(128)}, f32[40]{0:T(128)}, f32[40]{0:T(128)}) %tuple.33, (s32[40,128]{1,0:T(8,128)}, ...), branch_computations={%region_3.11_spmd, %region_11.12_spmd} | conditional | flops 24065960 | bytes 187456160 | solution.py:494
  18.6 0.6 copy.55
  19.2 0.7 broadcast_in_dim.18.params
  19.9 201.1 %branch_1_fun.2 = (f32[5,256,8,128]{3,2,1,0:T(8,128)}, f32[256,128]{1,0:T(8,128)}) custom-call(s32[5120]{0:T(1024)} %bitcast.14.tables, s32[1024]{0:T(1024)} %bitcast.74, f32[5,41,128]{2,1,0:T(8,128)} %broadcast_in_dim.18.params, f32[41,32768]{1,0:T(8,128)} %get-tuple-element.52.states), custom_call_target="tpu_custom_call" | custom-call | tf_op jit(solution)/shard_map/cond/branch_1_fun/pallas_call | solution.py:353
  221.1 8.4 %branch_1_fun.3 = f32[41,32768]{1,0:T(8,128)} custom-call(f32[5,256,8,128]{3,2,1,0:T(8,128)} %get-tuple-element.53.got, f32[256,128]{1,0:T(8,128)} %get-tuple-element.54.got_row, s32[256,128]{1,0:T(8,128)} %get-tuple-element.55.perm), custom_call_target="tpu_custom_call" | custom-call | tf_op jit(solution)/shard_map/cond/branch_1_fun/pallas_call | solution.py:408
  (2 shorter events, 0.0 us)
where the time goes:
time: 233 us; the launch traced here: 229 us
  Pallas kernels  221 us (95%)
  local copies, waits for them, and re-layouts  3.58 us (2%)
  other arithmetic  2.6 us (1%)
    pallas_call x1, Pallas kernels, exchange(): pl.pallas_call(functools.partial(exchange_kernel, peers, own_blocks, slot...  201 us
    pallas_call x1, Pallas kernels, gather_counts(): pl.pallas_call(functools.partial(counts_kernel, devices, peers), out_shap...  8.99 us
    pallas_call x1, Pallas kernels, place(): pl.pallas_call(functools.partial(place_kernel, tiles, step), grid=(own_bl...  8.35 us

commit v1 on v0

v1 whole, which is shorter than its diff:
```python
import functools
import jax
import jax.numpy as jnp
import numpy as np
from jax import lax
from jax.experimental import pallas as pl
from jax.experimental.pallas import tpu as pltpu
from jax.sharding import PartitionSpec as P

time_step = 0.25
LANES = 128
ROWS = 8
MESH_ID = pl.DeviceIdType.MESH
VMEM_LIMIT = 67043328
Z_STRIDE = 88
Z_NEAR = 88
P_STRIDE = 48
P_TABLE = 64
TIERS = ((72, 40), (80, 40), (88, 48))


def my_index(peers):
    return lax.axis_index("group") * peers + lax.axis_index("peer")


def counts_kernel(devices, peers, x_ref, out_ref, send_sem, recv_sem, local_sem):
    d = my_index(peers)
    barrier = pltpu.get_barrier_semaphore()
    for k in range(1, devices):
        to = (d + k) % devices
        pl.semaphore_signal(
            barrier, inc=1, device_id=(to // peers, to % peers), device_id_type=MESH_ID
        )
    pl.semaphore_wait(barrier, devices - 1)
    own = pltpu.make_async_copy(x_ref.at[0], out_ref.at[d], local_sem)
    own.start()
    for k in range(1, devices):
        to = (d + k) % devices
        pltpu.make_async_remote_copy(
            src_ref=x_ref.at[0], dst_ref=out_ref.at[d],
            send_sem=send_sem.at[k], recv_sem=recv_sem.at[k],
            device_id=(to // peers, to % peers), device_id_type=MESH_ID,
        ).start()
    own.wait()
    for k in range(1, devices):
        src = (d + devices - k) % devices
        pltpu.make_async_remote_copy(
            src_ref=x_ref.at[0], dst_ref=out_ref.at[src],
            send_sem=send_sem.at[k], recv_sem=recv_sem.at[k],
            device_id=(src // peers, src % peers), device_id_type=MESH_ID,
        ).wait()


def gather_counts(row, devices, peers):
    return pl.pallas_call(
        functools.partial(counts_kernel, devices, peers),
        out_shape=jax.ShapeDtypeStruct((devices, 1, LANES), jnp.int32),
        in_specs=[pl.BlockSpec(memory_space=pltpu.VMEM)],
        out_specs=pl.BlockSpec(memory_space=pltpu.VMEM),
        scratch_shapes=[
            pltpu.SemaphoreType.DMA((devices,)),
            pltpu.SemaphoreType.DMA((devices,)),
            pltpu.SemaphoreType.DMA,
        ],
        compiler_params=pltpu.CompilerParams(collective_id=0, has_side_effects=True),
    )(row)


def plane_of(d, peers):
    return (d // peers) * 2 + d % 2


def depth_of(d, peers):
    return (d % peers) // 2


def dot(a, b, contract=((1,), (0,))):
    return lax.dot_general(
        a, b, (contract, ((), ())), preferred_element_type=jnp.float32
    )


def iota(shape, axis):
    return lax.broadcasted_iota(jnp.int32, shape, axis)


def table_kernel(devices, peers, own_blocks, c_ref, part_ref, tab_ref, tier_ref):
    d = my_index(peers)
    plane = plane_of(d, peers)
    depth = depth_of(d, peers)
    planes = ROWS
    depths = peers // 2
    per = own_blocks // planes
    f32 = jnp.float32
    shift = ROWS - 1
    counts = c_ref[...].reshape(devices, LANES)
    lower = (iota((devices, devices), 1) < iota((devices, devices), 0)).astype(f32)
    starts = dot(lower, counts.astype(f32))
    starts_i = starts.astype(jnp.int32)
    upper = (
        iota((own_blocks, own_blocks), 0) < iota((own_blocks, own_blocks), 1)
    ).astype(f32)
    lane = iota((1, own_blocks), 1)
    lane_plane = lane // per
    stored = (lane % per) * planes + (plane ^ lane_plane)
    source_rows = iota((LANES, own_blocks), 0)
    row8 = iota((ROWS, own_blocks), 0)

    def classify(level):
        source = (lane_plane // 2) * peers + level * 2 + lane_plane % 2
        pick = (source_rows == source).astype(f32)
        begin = dot(starts, pick).astype(jnp.int32)
        dest = jnp.sum((begin <= stored).astype(jnp.int32), axis=0, keepdims=True) - 1
        level_to = depth_of(dest, peers)
        mask = (row8 == level_to).astype(f32)
        rank = jnp.sum(mask * dot(mask, upper), axis=0, keepdims=True).astype(jnp.int32)
        return dest, level_to, rank

    tab_ref[...] = jnp.zeros_like(tab_ref)
    _, level_to, rank = classify(depth)
    slots = iota((depths * LANES, own_blocks), 0)
    pick = (slots == level_to * LANES + rank).astype(f32)
    value = jnp.broadcast_to(lane, (ROWS, own_blocks)).astype(f32)
    got = dot(value, pick, ((1,), (1,))).astype(jnp.int32)
    for t in range(depths):
        tab_ref[t : t + 1, :] = got[0:1, t * LANES : (t + 1) * LANES]

    slots = iota((planes * P_TABLE, own_blocks), 0)
    before = jnp.zeros((ROWS, 1), f32)
    table = jnp.zeros((ROWS, planes * P_TABLE), f32)
    for level in range(depths):
        dest, level_to, rank = classify(level)
        here = level_to == depth
        plane_to = plane_of(dest, peers)
        mask = ((row8 == plane_to) & here).astype(f32)
        rank3 = jnp.sum(mask * (dot(mask, upper) + before), axis=0, keepdims=True)
        before = before + jnp.sum(mask, axis=1, keepdims=True)
        key = jnp.where(here, plane_to * P_TABLE + rank3.astype(jnp.int32), -1)
        pick = (slots == key).astype(f32)
        value = jnp.where(row8 == 0, rank, 1).astype(f32)
        got = dot(value, pick, ((1,), (1,)))
        table = table + got + float(level * Z_STRIDE) * got[1:2, :]
    table = table.astype(jnp.int32)
    table = jnp.clip(table, 0, depths * Z_STRIDE - 1)
    wide = planes * P_TABLE // LANES
    for t in range(wide):
        tab_ref[depths + t : depths + t + 1, :] = table[0:1, t * LANES : (t + 1) * LANES]

    part = part_ref[...]
    mine = iota((devices, LANES), 0) == d
    my_start = jnp.sum(jnp.where(mine, starts_i, 0), axis=0, keepdims=True)
    my_count = jnp.sum(jnp.where(mine, counts, 0), axis=0, keepdims=True)
    few = (iota((devices, own_blocks), 0) == part).astype(f32)
    rank = jnp.sum(few * dot(few, upper), axis=0, keepdims=True).astype(jnp.int32)
    pick = (source_rows == part).astype(f32)
    start8 = jnp.broadcast_to(my_start, (ROWS, LANES))
    begin = dot(start8.astype(f32), pick).astype(jnp.int32)[0:1]
    at = begin + rank
    part_plane = plane_of(part, peers)
    middle = (at % planes) ^ part_plane
    ids = iota((1, LANES), 1)
    residue = iota((ROWS, LANES), 0) ^ plane_of(ids, peers)
    in_use = ids < devices
    share = ((start8 + my_count + (shift - residue)) // planes) - (
        (start8 + (shift - residue)) // planes
    )
    share = jnp.where(in_use, share, 0)

    def order_of(p):
        return jnp.where(
            p < devices, depth_of(p, peers) * planes + plane_of(p, peers), LANES
        )

    ahead = (
        order_of(iota((LANES, LANES), 0)) < order_of(iota((LANES, LANES), 1))
    ).astype(f32)
    base = dot(share.astype(f32), ahead)
    base = dot(base, pick)
    base = jnp.sum(jnp.where(row8 == middle, base, 0.0), axis=0, keepdims=True)
    first = (begin + (shift - at % planes)) // planes
    final = middle * P_STRIDE + base.astype(jnp.int32) + at // planes - first
    final = jnp.clip(final, 0, planes * P_STRIDE - 1)
    row = depths + wide
    for t in range(own_blocks // LANES):
        tab_ref[row + t : row + t + 1, :] = final[:, t * LANES : (t + 1) * LANES]

    by_slab = (
        depth_of(iota((ROWS, devices), 1), peers) == iota((ROWS, devices), 0)
    ).astype(f32)
    rows = iota((LANES, LANES), 0)
    by_part = (
        (depth_of(rows, peers) == iota((LANES, LANES), 1)) & (rows < devices)
    ).astype(f32)
    far = ((iota((ROWS, LANES), 0) ^ iota((ROWS, LANES), 1)) & 2) != 0
    level_most = jnp.zeros((ROWS, LANES), f32)
    plane_most = jnp.zeros((devices, 1), f32)
    for k in range(planes):
        left = shift - (k ^ plane_of(ids, peers))
        some = (starts_i + counts + left) // planes - (starts_i + left) // planes
        some = jnp.where(in_use, some, 0).astype(f32)
        plane_most = jnp.maximum(plane_most, jnp.sum(some, axis=1, keepdims=True))
        level_most = jnp.maximum(level_most, dot(dot(by_slab, some), by_part))
    used = jnp.max(jnp.where(far, level_most, 0.0)).astype(jnp.int32)
    most = jnp.max(level_most).astype(jnp.int32)
    final_most = jnp.max(plane_most).astype(jnp.int32)
    tier = jnp.int32(len(TIERS))
    for t in range(len(TIERS) - 1, -1, -1):
        room, room3 = TIERS[t]
        fits = (used <= room) & (final_most <= room3) & (most <= Z_NEAR)
        tier = jnp.where(fits, t, tier)
    tier_ref[0] = tier


def make_tables(counts, part, devices, peers, own_blocks):
    return pl.pallas_call(
        functools.partial(table_kernel, devices, peers, own_blocks),
        out_shape=(
            jax.ShapeDtypeStruct((2 * ROWS, LANES), jnp.int32),
            jax.ShapeDtypeStruct((1,), jnp.int32),
        ),
        in_specs=[
            pl.BlockSpec(memory_space=pltpu.VMEM),
            pl.BlockSpec(memory_space=pltpu.VMEM),
        ],
        out_specs=(
            pl.BlockSpec(memory_space=pltpu.VMEM),
            pl.BlockSpec(memory_space=pltpu.SMEM),
        ),
    )(counts, part)


def exchange_kernel(peers, own_blocks, tiles, rooms, tables, params, states, out, out_row, *refs):
    d = my_index(peers)
    plane = plane_of(d, peers)
    depth = depth_of(d, peers)
    planes = ROWS
    depths = peers // 2
    per = own_blocks // planes
    chunks = tiles + 1
    unroll = 8
    own, own_row = refs[0:2]
    at = 2
    groups = []
    for _ in range(6):
        groups.append(refs[at : at + chunks])
        at += chunks
    landed1, packed2, landed2, packed3, landed3, ready = groups
    send_sem, recv_sem, out_sem = refs[at:]
    room2 = (None, Z_NEAR, rooms[0], rooms[0])
    room3 = rooms[1]
    wide = planes * P_TABLE // LANES

    def device(to_plane, to_depth):
        return (to_plane // 2, to_depth * 2 + to_plane % 2)

    barrier = pltpu.get_barrier_semaphore()
    partners = [device(plane ^ m, depth) for m in range(1, planes)]
    partners += [device(plane, depth ^ m) for m in range(1, depths)]
    for to in partners:
        pl.semaphore_signal(barrier, inc=1, device_id=to, device_id_type=MESH_ID)

    def advance_block(i, u):
        cols = pl.ds(pl.multiple_of((i * planes + u) * LANES, LANES), LANES)
        top = states[0:ROWS, cols]
        voltage = top[0:1, :]
        spread = jnp.broadcast_to(voltage, (ROWS, LANES))
        slow = -(1.0 + jax.nn.sigmoid(spread))

        def gates(vals, base, count):
            half, steep, rate, cond, rev = (
                params[k, base : base + count, :] for k in range(5)
            )
            v = spread[0:count]
            steady = jax.nn.sigmoid((v - half) * steep)
            damping = jnp.exp(rate * slow[0:count])
            new = steady + (vals - steady) * damping
            return new, cond * new * (v - rev)

        def put(c, value):
            if u == 0:
                landed1[c][plane * per + i] = value
            else:
                own[c, u - 1, i] = value

        total = jnp.zeros((ROWS, LANES), jnp.float32)
        for t in range(1, tiles):
            new, term = gates(states[t * ROWS : (t + 1) * ROWS, cols], t * ROWS, ROWS)
            put(t, new)
            total = total + term
        last = tiles * ROWS
        new_row, term_row = gates(states[last : last + 1, cols], last, 1)
        if u == 0:
            landed1[tiles][pl.ds(plane * per + i, 1), :] = new_row
        else:
            own_row[u - 1, pl.ds(i, 1), :] = new_row
        new, term = gates(top, 0, ROWS)
        total = total + term
        current = jnp.sum(total, axis=0, keepdims=True) + term_row
        moved = voltage - time_step * current
        first = lax.broadcasted_iota(jnp.int32, (ROWS, LANES), 0) == 0
        put(0, jnp.where(first, jnp.broadcast_to(moved, (ROWS, LANES)), new))

    def advance_loop(i, _):
        for u in range(planes):
            advance_block(i, u)
        return 0

    lax.fori_loop(0, per, advance_loop, 0)
    pl.semaphore_wait(barrier, len(partners))

    copies = {}

    def send(c, phase, m, src, dst, to):
        copy = pltpu.make_async_remote_copy(
            src_ref=src,
            dst_ref=dst,
            send_sem=send_sem.at[c, phase, m],
            recv_sem=recv_sem.at[c, phase, m],
            device_id=to,
            device_id_type=MESH_ID,
        )
        copy.start()
        copies[(c, phase, m)] = copy

    def gather(c, count, table_row, table_col, src, put, first):
        def body(i, _):
            for u in range(unroll):
                k = i * unroll + u
                where = tables[table_row, table_col + k]
                if c < tiles:
                    put[first + k] = src[where]
                else:
                    put[pl.ds(first + k, 1), :] = src[pl.ds(where, 1), :]
            return 0

        lax.fori_loop(0, count // unroll, body, 0)

    def phase1(c):
        source = own.at[c] if c < tiles else own_row
        for m in range(1, planes):
            send(
                c, 0, m, source.at[m - 1], landed1[c].at[pl.ds(plane * per, per)],
                device(plane ^ m, depth),
            )

    def phase2(c):
        for m in range(1, planes):
            copies[(c, 0, m)].wait_recv()
        for m in (2, 3, 1):
            gather(c, room2[m], depth ^ m, 0, landed1[c], packed2[c].at[m - 1], 0)
            send(
                c, 1, m, packed2[c].at[m - 1, pl.ds(0, room2[m])],
                landed2[c].at[pl.ds(depth * Z_STRIDE, room2[m])],
                device(plane, depth ^ m),
            )
        gather(c, Z_NEAR, depth, 0, landed1[c], landed2[c], depth * Z_STRIDE)

    def phase3(c):
        for m in range(1, depths):
            copies[(c, 1, m)].wait_recv()
        for m in (6, 7, 4, 5, 1, 3, 2):
            to = plane ^ m
            gather(
                c, room3, depths + to // 2, (to % 2) * P_TABLE,
                landed2[c], packed3[c].at[m - 1], 0,
            )
            send(
                c, 2, m, packed3[c].at[m - 1, pl.ds(0, room3)],
                landed3[c].at[pl.ds(plane * P_STRIDE, room3)],
                device(to, depth),
            )
        gather(
            c, room3, depths + plane // 2, (plane % 2) * P_TABLE,
            landed2[c], landed3[c], plane * P_STRIDE,
        )

    outs = []

    def finish(c):
        for m in range(1, planes):
            copies[(c, 2, m)].wait_recv()
        for t in range(own_blocks // LANES):
            gather(c, LANES, depths + wide + t, 0, landed3[c], ready[c], t * LANES)
        copy = pltpu.make_async_copy(
            ready[c], out.at[c] if c < tiles else out_row, out_sem.at[c]
        )
        copy.start()
        outs.append(copy)

    for phase, c in EVENTS:
        (phase1, phase2, phase3, finish)[phase](c)
    for copy in outs:
        copy.wait()
    for copy in copies.values():
        copy.wait_send()


EVENTS = (
    (0, 0), (0, 1), (0, 2), (0, 3), (1, 0), (1, 1), (1, 2), (2, 0), (0, 4), (0, 5), (1, 3),
    (2, 1), (1, 4), (1, 5), (3, 0), (2, 2), (3, 1), (2, 3), (3, 2), (2, 4), (2, 5), (3, 3),
    (3, 4), (3, 5),
)


def exchange(tables, params, states, peers, own_blocks, rooms):
    tiles = states.shape[0] // ROWS
    planes = ROWS
    depths = peers // 2
    per = own_blocks // planes
    f32 = jnp.float32

    def buffers(*lead):
        kinds = [pltpu.VMEM(lead + (ROWS, LANES), f32) for _ in range(tiles)]
        return kinds + [pltpu.VMEM(lead + (LANES,), f32)]

    return pl.pallas_call(
        functools.partial(exchange_kernel, peers, own_blocks, tiles, rooms),
        out_shape=(
            jax.ShapeDtypeStruct((tiles, own_blocks, ROWS, LANES), f32),
            jax.ShapeDtypeStruct((own_blocks, LANES), f32),
        ),
        in_specs=[
            pl.BlockSpec(memory_space=pltpu.SMEM),
            pl.BlockSpec(memory_space=pltpu.VMEM),
            pl.BlockSpec(memory_space=pltpu.VMEM),
        ],
        out_specs=(
            pl.BlockSpec(memory_space=pl.ANY),
            pl.BlockSpec(memory_space=pl.ANY),
        ),
        scratch_shapes=[
            pltpu.VMEM((tiles, planes - 1, per, ROWS, LANES), f32),
            pltpu.VMEM((planes - 1, per, LANES), f32),
            *buffers(own_blocks),
            *buffers(depths - 1, Z_STRIDE),
            *buffers(depths * Z_STRIDE),
            *buffers(planes - 1, P_STRIDE),
            *buffers(planes * P_STRIDE),
            *buffers(own_blocks),
            pltpu.SemaphoreType.DMA((tiles + 1, 3, planes)),
            pltpu.SemaphoreType.DMA((tiles + 1, 3, planes)),
            pltpu.SemaphoreType.DMA((tiles + 1,)),
        ],
        compiler_params=pltpu.CompilerParams(
            collective_id=1 + TIERS.index(rooms),
            has_side_effects=True,
            vmem_limit_bytes=VMEM_LIMIT,
        ),
    )(tables, params, states)


def place_kernel(tiles, blocks, got, got_row, perm, out):
    for group in range(blocks // ROWS):
        rows = slice(group * ROWS, (group + 1) * ROWS)
        turned = jnp.take_along_axis(
            got_row[rows, :], perm[rows, :], axis=1, mode="promise_in_bounds"
        )
        for u in range(ROWS):
            b = group * ROWS + u
            cols = slice(b * LANES, (b + 1) * LANES)
            where = jnp.broadcast_to(perm[b : b + 1, :], (ROWS, LANES))
            for t in range(tiles):
                out[t * ROWS : (t + 1) * ROWS, cols] = jnp.take_along_axis(
                    got[t, b], where, axis=1, mode="promise_in_bounds"
                )
            out[tiles * ROWS : tiles * ROWS + 1, cols] = turned[u : u + 1, :]


def place(got, got_row, perm, width, own_blocks):
    tiles = got.shape[0]
    step = 32
    return pl.pallas_call(
        functools.partial(place_kernel, tiles, step),
        grid=(own_blocks // step,),
        out_shape=jax.ShapeDtypeStruct((width, own_blocks * LANES), jnp.float32),
        in_specs=[
            pl.BlockSpec((tiles, step, ROWS, LANES), lambda i: (0, i, 0, 0)),
            pl.BlockSpec((step, LANES), lambda i: (i, 0)),
            pl.BlockSpec((step, LANES), lambda i: (i, 0)),
        ],
        out_specs=pl.BlockSpec((width, step * LANES), lambda i: (0, i)),
    )(got, got_row, perm)


def advance(state_rows, half_volt, steepness, gate_rate, conductance, reversal):
    voltage = state_rows[0:1]
    gate_vals = state_rows[1:]
    steady = jax.nn.sigmoid((voltage - half_volt[:, None]) * steepness[:, None])
    damping = jnp.exp(-gate_rate[:, None] * (1.0 + jax.nn.sigmoid(voltage)))
    gate_vals = steady + (gate_vals - steady) * damping
    current = jnp.sum(
        conductance[:, None] * gate_vals * (voltage - reversal[:, None]), axis=0, keepdims=True
    )
    voltage = voltage - time_step * current
    return jnp.concatenate([voltage, gate_vals], axis=0)


def general(counts_all, devices, states, block_part, tile_perm, *gate_params):
    d = lax.axis_index(("group", "peer"))
    local_blocks = block_part.shape[0]
    tile_width = tile_perm.shape[1]
    width = states.shape[0]
    capacity = 2 * local_blocks // devices
    partitions = jnp.arange(devices, dtype=jnp.int32)
    onehot = (block_part[:, None] == partitions[None, :]).astype(jnp.int32)
    before = (partitions < d).astype(jnp.int32)
    earlier = jnp.sum(counts_all * before[:, None], axis=0, dtype=jnp.int32)
    rank_in = jnp.sum(
        (jnp.cumsum(onehot, axis=0, dtype=jnp.int32) - onehot) * onehot, axis=1, dtype=jnp.int32
    )
    local_index = jnp.sum(onehot * earlier[None, :], axis=1, dtype=jnp.int32) + rank_in
    slot_index = block_part * capacity + rank_in
    requests = jnp.full((devices * capacity,), -1, jnp.int32).at[slot_index].set(local_index)
    requests = requests.reshape(devices, capacity)
    advanced = advance(states, *gate_params)
    advanced = advanced.reshape(width, local_blocks, tile_width)
    wanted = lax.all_to_all(requests, ("group", "peer"), split_axis=0, concat_axis=0, tiled=True)
    picked = jnp.maximum(wanted, 0).reshape(-1)
    served = jnp.take(advanced, picked, axis=1)
    arrived = lax.all_to_all(
        served.reshape(width, wanted.shape[0], wanted.shape[1], tile_width),
        ("group", "peer"), split_axis=1, concat_axis=1, tiled=True,
    )
    flat_cols = (slot_index[:, None] * tile_width + tile_perm).reshape(-1)
    return jnp.take(arrived.reshape(width, devices * capacity * tile_width), flat_cols, axis=1)


def on_device(devices, peers, states, block_part, tile_perm, *gate_params):
    own_blocks = block_part.shape[0]
    width = states.shape[0]
    partitions = jnp.arange(LANES, dtype=jnp.int32)
    counts = jnp.sum(
        (block_part[:, None] == partitions[None, :]).astype(jnp.int32), axis=0, dtype=jnp.int32
    )
    if (devices, peers) != (4 * ROWS, ROWS) or width % ROWS != 1:
        gathered = lax.all_gather(counts[:devices], ("group", "peer"))
        return general(gathered, devices, states, block_part, tile_perm, *gate_params)
    gathered = gather_counts(counts.reshape(1, 1, LANES), devices, peers)
    tables, tier = make_tables(
        gathered, block_part.reshape(1, own_blocks), devices, peers, own_blocks
    )
    padded = jnp.stack([jnp.pad(p, (1, 0)) for p in gate_params])
    params = jnp.broadcast_to(padded[:, :, None], padded.shape + (LANES,))

    def fast(rooms):
        got, got_row = exchange(tables, params, states, peers, own_blocks, rooms)
        return place(got, got_row, tile_perm, width, own_blocks)

    def slow():
        matrix = gathered[:, 0, :devices]
        return general(matrix, devices, states, block_part, tile_perm, *gate_params)

    choices = [functools.partial(fast, rooms) for rooms in TIERS] + [slow]
    return lax.switch(tier[0], choices)


def solution(mesh):
    both = P(("group", "peer"))
    return jax.shard_map(
        functools.partial(on_device, mesh.devices.size, mesh.shape["peer"]),
        mesh=mesh,
        in_specs=(P(None, ("group", "peer")), both, P(("group", "peer"), None)) + (P(),) * 5,
        out_specs=P(None, ("group", "peer")),
        check_vma=False,
    )
```

time: 233 us -> 201 us (0.86); the launches traced: 229 us -> 201 us
  Pallas kernels: 221 us -> 196 us
    pallas_call x1, Pallas kernels: 201 us -> 175 us  [exchange(): pl.pallas_call(functools.partial(exchange_kernel, peers, own_blocks, tile...]
where the time goes in v1:
time: 201 us
  Pallas kernels  196 us (98%)
  local copies, waits for them, and re-layouts  2.99 us (1%)
    pallas_call x1, Pallas kernels, exchange(): pl.pallas_call(functools.partial(exchange_kernel, peers, own_blocks, tile...  175 us
    pallas_call x1, Pallas kernels, gather_counts(): pl.pallas_call(functools.partial(counts_kernel, devices, peers), out_shap...  8.99 us
    pallas_call x1, Pallas kernels, place(): pl.pallas_call(functools.partial(place_kernel, tiles, step), grid=(own_bl...  8.35 us

profile of v1, /device:TPU:9, one launch (start us, length us, event | category | flops | bytes accessed | tf_op | source)
XLA Modules:
  0.0 200.9 jit_solution(1336229336643244413)
XLA Ops:
  0.0 0.7 pad_bitcast_fusion.4
  0.7 1.3 convert_reduce_fusion
  2.0 0.7 pad_bitcast_fusion.2
  2.8 0.7 pad_bitcast_fusion
  3.6 9.0 %shard_map.86.c_ref = s32[32,1,128]{2,1,0:T(1,128)S(1)} custom-call(s32[1,1,128]{2,1,0:T(1,128)} %bitcast.71), custom_call_target="tpu_custom_call" | custom-call | tf_op jit(solution)/shard_map/pallas_call | solution.py:55
  12.5 3.5 %shard_map.87 = (s32[16,128]{1,0:T(8,128)}, s32[1]{0:T(128)}) custom-call(s32[32,1,128]{2,1,0:T(1,128)S(1)} %shard_map.86.c_ref, s32[1,256]{1,0:T(1,128)} %bitcast.69), custom_call_target="tpu_custom_call" | custom-call | tf_op jit(solution)/shard_map/pallas_call | solution.py:215
  16.7 184.2 %conditional.1 = (f32[41,32768]{1,0:T(8,128)}) conditional(s32[]{:T(128)} %bitcast.18, (f32[5,41]{1,0:T(8,128)S(1)}, s32[16,128]{1,0:T(8,128)}, f32[41,32768]{1,0:T(8,128)}, s32[256,128]{1,0:T(8,128)}) %tuple.17, (f32[5,41]{1,0:T(8,128)S(1)}, s32[16,128]{1,0:T(8,128)}, f32[41,32768]{1,0:T(8,128)}, ...), branch_computations={%region_1.2_spmd, %region_2.3_spmd, %region_3.4_spmd, %region_4.12... | conditional | flops 24065960 | bytes 187521728 | solution.py:554
  16.7 0.7 broadcast_in_dim.17.params
  17.5 175.1 %branch_0_fun.2 = (f32[5,256,8,128]{3,2,1,0:T(8,128)}, f32[256,128]{1,0:T(8,128)}) custom-call(s32[16,128]{1,0:T(8,128)} %get-tuple-element.55.tables, f32[5,41,128]{2,1,0:T(8,128)} %broadcast_in_dim.17.params, f32[41,32768]{1,0:T(8,128)} %get-tuple-element.57.states), custom_call_target="tpu_custom_call" | custom-call | tf_op jit(solution)/shard_map/cond/branch_0_fun/pallas_call | solution.py:416
  192.6 8.4 %branch_0_fun.3 = f32[41,32768]{1,0:T(8,128)} custom-call(f32[5,256,8,128]{3,2,1,0:T(8,128)} %get-tuple-element.58.got, f32[256,128]{1,0:T(8,128)} %get-tuple-element.59.got_row, s32[256,128]{1,0:T(8,128)} %get-tuple-element.60.perm), custom_call_target="tpu_custom_call" | custom-call | tf_op jit(solution)/shard_map/cond/branch_0_fun/pallas_call | solution.py:472
  (1 shorter events, 0.0 us)

commit v2 on v1

--- a/solution.py
+++ b/solution.py
@@ -16,54 +16,12 @@
 Z_NEAR = 88
 P_STRIDE = 48
 P_TABLE = 64
+PIECES = 4
 TIERS = ((72, 40), (80, 40), (88, 48))
 
 
 def my_index(peers):
     return lax.axis_index("group") * peers + lax.axis_index("peer")
-
-
-def counts_kernel(devices, peers, x_ref, out_ref, send_sem, recv_sem, local_sem):
-    d = my_index(peers)
-    barrier = pltpu.get_barrier_semaphore()
-    for k in range(1, devices):
-        to = (d + k) % devices
-        pl.semaphore_signal(
-            barrier, inc=1, device_id=(to // peers, to % peers), device_id_type=MESH_ID
-        )
-    pl.semaphore_wait(barrier, devices - 1)
-    own = pltpu.make_async_copy(x_ref.at[0], out_ref.at[d], local_sem)
-    own.start()
-    for k in range(1, devices):
-        to = (d + k) % devices
-        pltpu.make_async_remote_copy(
-            src_ref=x_ref.at[0], dst_ref=out_ref.at[d],
-            send_sem=send_sem.at[k], recv_sem=recv_sem.at[k],
-            device_id=(to // peers, to % peers), device_id_type=MESH_ID,
-        ).start()
-    own.wait()
-    for k in range(1, devices):
-        src = (d + devices - k) % devices
-        pltpu.make_async_remote_copy(
-            src_ref=x_ref.at[0], dst_ref=out_ref.at[src],
-            send_sem=send_sem.at[k], recv_sem=recv_sem.at[k],
-            device_id=(src // peers, src % peers), device_id_type=MESH_ID,
-        ).wait()
-
-
-def gather_counts(row, devices, peers):
-    return pl.pallas_call(
-        functools.partial(counts_kernel, devices, peers),
-        out_shape=jax.ShapeDtypeStruct((devices, 1, LANES), jnp.int32),
-        in_specs=[pl.BlockSpec(memory_space=pltpu.VMEM)],
-        out_specs=pl.BlockSpec(memory_space=pltpu.VMEM),
-        scratch_shapes=[
-            pltpu.SemaphoreType.DMA((devices,)),
-            pltpu.SemaphoreType.DMA((devices,)),
-            pltpu.SemaphoreType.DMA,
-        ],
-        compiler_params=pltpu.CompilerParams(collective_id=0, has_side_effects=True),
-    )(row)
 
 
 def plane_of(d, peers):
@@ -84,7 +42,7 @@
     return lax.broadcasted_iota(jnp.int32, shape, axis)
 
 
-def table_kernel(devices, peers, own_blocks, c_ref, part_ref, tab_ref, tier_ref):
+def fill_tables(devices, peers, own_blocks, c_ref, part_ref, tab_ref, tier_ref):
     d = my_index(peers)
     plane = plane_of(d, peers)
     depth = depth_of(d, peers)
@@ -211,53 +169,48 @@
     tier_ref[0] = tier
 
 
-def make_tables(counts, part, devices, peers, own_blocks):
-    return pl.pallas_call(
-        functools.partial(table_kernel, devices, peers, own_blocks),
-        out_shape=(
-            jax.ShapeDtypeStruct((2 * ROWS, LANES), jnp.int32),
-            jax.ShapeDtypeStruct((1,), jnp.int32),
-        ),
-        in_specs=[
-            pl.BlockSpec(memory_space=pltpu.VMEM),
-            pl.BlockSpec(memory_space=pltpu.VMEM),
-        ],
-        out_specs=(
-            pl.BlockSpec(memory_space=pltpu.VMEM),
-            pl.BlockSpec(memory_space=pltpu.SMEM),
-        ),
-    )(counts, part)
-
-
-def exchange_kernel(peers, own_blocks, tiles, rooms, tables, params, states, out, out_row, *refs):
+def opening_kernel(
+    devices, peers, own_blocks, tiles,
+    part_ref, half_ref, steep_ref, rate_ref, cond_ref, rev_ref, states_ref,
+    tab_ref, tier_ref, counts_out, own_out, row_out, first_out,
+    states, params, own, own_row, landed, tally, counts,
+    load_sem, count_send, count_recv, send_sem, recv_sem, out_sem,
+):
     d = my_index(peers)
     plane = plane_of(d, peers)
     depth = depth_of(d, peers)
     planes = ROWS
-    depths = peers // 2
     per = own_blocks // planes
-    chunks = tiles + 1
-    unroll = 8
-    own, own_row = refs[0:2]
-    at = 2
-    groups = []
-    for _ in range(6):
-        groups.append(refs[at : at + chunks])
-        at += chunks
-    landed1, packed2, landed2, packed3, landed3, ready = groups
-    send_sem, recv_sem, out_sem = refs[at:]
-    room2 = (None, Z_NEAR, rooms[0], rooms[0])
-    room3 = rooms[1]
-    wide = planes * P_TABLE // LANES
-
-    def device(to_plane, to_depth):
-        return (to_plane // 2, to_depth * 2 + to_plane % 2)
+    step = per // PIECES
+    width = step * planes * LANES
+
+    loads = []
+    for q in range(PIECES):
+        cols = pl.ds(q * width, width)
+        copy = pltpu.make_async_copy(
+            states_ref.at[:, cols], states.at[:, cols], load_sem.at[q]
+        )
+        copy.start()
+        loads.append(copy)
 
     barrier = pltpu.get_barrier_semaphore()
-    partners = [device(plane ^ m, depth) for m in range(1, planes)]
-    partners += [device(plane, depth ^ m) for m in range(1, depths)]
-    for to in partners:
-        pl.semaphore_signal(barrier, inc=1, device_id=to, device_id_type=MESH_ID)
+    for k in range(1, devices):
+        to = (d + k) % devices
+        pl.semaphore_signal(
+            barrier, inc=1, device_id=(to // peers, to % peers), device_id_type=MESH_ID
+        )
+
+    match = (iota((LANES, own_blocks), 0) == part_ref[...]).astype(jnp.float32)
+    ones = jnp.ones((ROWS, own_blocks), jnp.float32)
+    tally[...] = dot(ones, match, ((1,), (1,)))[0:1].astype(jnp.int32)
+    counts[d] = tally[...]
+    gates_all = half_ref.shape[1]
+    for k, ref in enumerate((half_ref, steep_ref, rate_ref, cond_ref, rev_ref)):
+        for base in range(0, tiles * ROWS + ROWS, ROWS):
+            shape = (ROWS, gates_all)
+            chosen = iota(shape, 1) == iota(shape, 0) + (base - 1)
+            column = jnp.sum(jnp.where(chosen, ref[...], 0.0), axis=1, keepdims=True)
+            params[k, base : base + ROWS, :] = jnp.broadcast_to(column, (ROWS, LANES))
 
     def advance_block(i, u):
         cols = pl.ds(pl.multiple_of((i * planes + u) * LANES, LANES), LANES)
@@ -276,36 +229,165 @@
             new = steady + (vals - steady) * damping
             return new, cond * new * (v - rev)
 
-        def put(c, value):
-            if u == 0:
-                landed1[c][plane * per + i] = value
-            else:
-                own[c, u - 1, i] = value
-
         total = jnp.zeros((ROWS, LANES), jnp.float32)
         for t in range(1, tiles):
             new, term = gates(states[t * ROWS : (t + 1) * ROWS, cols], t * ROWS, ROWS)
-            put(t, new)
+            own[t - 1, u, i] = new
             total = total + term
         last = tiles * ROWS
         new_row, term_row = gates(states[last : last + 1, cols], last, 1)
-        if u == 0:
-            landed1[tiles][pl.ds(plane * per + i, 1), :] = new_row
-        else:
-            own_row[u - 1, pl.ds(i, 1), :] = new_row
+        own_row[u, pl.ds(i, 1), :] = new_row
         new, term = gates(top, 0, ROWS)
         total = total + term
         current = jnp.sum(total, axis=0, keepdims=True) + term_row
         moved = voltage - time_step * current
         first = lax.broadcasted_iota(jnp.int32, (ROWS, LANES), 0) == 0
-        put(0, jnp.where(first, jnp.broadcast_to(moved, (ROWS, LANES)), new))
+        value = jnp.where(first, jnp.broadcast_to(moved, (ROWS, LANES)), new)
+        if u == 0:
+            landed[plane * per + i] = value
+        else:
+            own[tiles - 1, u, i] = value
 
     def advance_loop(i, _):
         for u in range(planes):
             advance_block(i, u)
         return 0
 
-    lax.fori_loop(0, per, advance_loop, 0)
+    sends = []
+    outs = []
+    count_copies = []
+    for q in range(PIECES):
+        loads[q].wait()
+        lax.fori_loop(q * step, (q + 1) * step, advance_loop, 0)
+        if q == 0:
+            pl.semaphore_wait(barrier, devices - 1)
+            for k in range(1, devices):
+                to = (d + k) % devices
+                copy = pltpu.make_async_remote_copy(
+                    src_ref=tally, dst_ref=counts.at[d],
+                    send_sem=count_send.at[k], recv_sem=count_recv.at[k],
+                    device_id=(to // peers, to % peers), device_id_type=MESH_ID,
+                )
+                copy.start()
+                count_copies.append(copy)
+        for m in (6, 7, 4, 5, 1, 3, 2):
+            to = plane ^ m
+            copy = pltpu.make_async_remote_copy(
+                src_ref=own.at[tiles - 1, m, pl.ds(q * step, step)],
+                dst_ref=landed.at[pl.ds(plane * per + q * step, step)],
+                send_sem=send_sem.at[q, m], recv_sem=recv_sem.at[q, m],
+                device_id=(to // 2, depth * 2 + to % 2), device_id_type=MESH_ID,
+            )
+            copy.start()
+            sends.append(copy)
+        some = pl.ds(q * step, step)
+        copy = pltpu.make_async_copy(
+            own.at[pl.ds(0, tiles - 1), :, some], own_out.at[:, :, some], out_sem.at[q, 0]
+        )
+        copy.start()
+        outs.append(copy)
+        copy = pltpu.make_async_copy(
+            own_row.at[:, some], row_out.at[:, some], out_sem.at[q, 1]
+        )
+        copy.start()
+        outs.append(copy)
+    for copy in count_copies:
+        copy.wait_recv()
+    counts_out[...] = counts[...]
+    fill_tables(devices, peers, own_blocks, counts, part_ref, tab_ref, tier_ref)
+    for copy in sends:
+        copy.wait_recv()
+    copy = pltpu.make_async_copy(landed, first_out, out_sem.at[PIECES, 0])
+    copy.start()
+    outs.append(copy)
+    for copy in count_copies + sends:
+        copy.wait_send()
+    for copy in outs:
+        copy.wait()
+
+
+def opening(part, gate_params, states, devices, peers):
+    own_blocks = part.shape[1]
+    tiles = states.shape[0] // ROWS
+    planes = ROWS
+    per = own_blocks // planes
+    f32 = jnp.float32
+    vmem = pl.BlockSpec(memory_space=pltpu.VMEM)
+    anywhere = pl.BlockSpec(memory_space=pl.ANY)
+    return pl.pallas_call(
+        functools.partial(opening_kernel, devices, peers, own_blocks, tiles),
+        out_shape=(
+            jax.ShapeDtypeStruct((2 * ROWS, LANES), jnp.int32),
+            jax.ShapeDtypeStruct((1,), jnp.int32),
+            jax.ShapeDtypeStruct((devices, 1, LANES), jnp.int32),
+            jax.ShapeDtypeStruct((tiles - 1, planes, per, ROWS, LANES), f32),
+            jax.ShapeDtypeStruct((planes, per, LANES), f32),
+            jax.ShapeDtypeStruct((own_blocks, ROWS, LANES), f32),
+        ),
+        in_specs=[vmem] * 6 + [anywhere],
+        out_specs=(
+            vmem, pl.BlockSpec(memory_space=pltpu.SMEM), vmem, anywhere, anywhere, anywhere,
+        ),
+        scratch_shapes=[
+            pltpu.VMEM(states.shape, f32),
+            pltpu.VMEM((5, (tiles + 1) * ROWS, LANES), f32),
+            pltpu.VMEM((tiles, planes, per, ROWS, LANES), f32),
+            pltpu.VMEM((planes, per, LANES), f32),
+            pltpu.VMEM((own_blocks, ROWS, LANES), f32),
+            pltpu.VMEM((1, LANES), jnp.int32),
+            pltpu.VMEM((devices, 1, LANES), jnp.int32),
+            pltpu.SemaphoreType.DMA((PIECES,)),
+            pltpu.SemaphoreType.DMA((devices,)),
+            pltpu.SemaphoreType.DMA((devices,)),
+            pltpu.SemaphoreType.DMA((PIECES, planes)),
+            pltpu.SemaphoreType.DMA((PIECES, planes)),
+            pltpu.SemaphoreType.DMA((PIECES + 1, 2)),
+        ],
+        compiler_params=pltpu.CompilerParams(
+            collective_id=0, has_side_effects=True, vmem_limit_bytes=VMEM_LIMIT
+        ),
+    )(part, *gate_params, states)
+
+
+def exchange_kernel(peers, own_blocks, tiles, rooms, tables, own, own_row, ahead, out, out_row, *refs):
+    d = my_index(peers)
+    plane = plane_of(d, peers)
+    depth = depth_of(d, peers)
+    planes = ROWS
+    depths = peers // 2
+    per = own_blocks // planes
+    chunks = tiles + 1
+    unroll = 8
+    at = 0
+    groups = []
+    for _ in range(6):
+        groups.append(refs[at : at + chunks])
+        at += chunks
+    landed1, packed2, landed2, packed3, landed3, ready = groups
+    send_sem, recv_sem, out_sem, in_sem = refs[at:]
+    room2 = (None, Z_NEAR, rooms[0], rooms[0])
+    room3 = rooms[1]
+    wide = planes * P_TABLE // LANES
+
+    def device(to_plane, to_depth):
+        return (to_plane // 2, to_depth * 2 + to_plane % 2)
+
+    barrier = pltpu.get_barrier_semaphore()
+    partners = [device(plane ^ m, depth) for m in range(1, planes)]
+    partners += [device(plane, depth ^ m) for m in range(1, depths)]
+    for to in partners:
+        pl.semaphore_signal(barrier, inc=1, device_id=to, device_id_type=MESH_ID)
+
+    loads = [pltpu.make_async_copy(ahead, landed1[0], in_sem.at[0])]
+    for c in range(1, chunks):
+        source = own.at[c - 1, 0] if c < tiles else own_row.at[0]
+        loads.append(
+            pltpu.make_async_copy(
+                source, landed1[c].at[pl.ds(plane * per, per)], in_sem.at[c]
+            )
+        )
+    for copy in loads:
+        copy.start()
     pl.semaphore_wait(barrier, len(partners))
 
     copies = {}
@@ -336,15 +418,16 @@
         lax.fori_loop(0, count // unroll, body, 0)
 
     def phase1(c):
-        source = own.at[c] if c < tiles else own_row
-        for m in range(1, planes):
+        source = own.at[c - 1] if c < tiles else own_row
+        for m in (6, 7, 4, 5, 1, 3, 2):
             send(
-                c, 0, m, source.at[m - 1], landed1[c].at[pl.ds(plane * per, per)],
+                c, 0, m, source.at[m], landed1[c].at[pl.ds(plane * per, per)],
                 device(plane ^ m, depth),
             )
 
     def phase2(c):
-        for m in range(1, planes):
+        loads[c].wait()
+        for m in range(1, planes if c else 1):
             copies[(c, 0, m)].wait_recv()
         for m in (2, 3, 1):
             gather(c, room2[m], depth ^ m, 0, landed1[c], packed2[c].at[m - 1], 0)
@@ -396,14 +479,14 @@
 
 
 EVENTS = (
-    (0, 0), (0, 1), (0, 2), (0, 3), (1, 0), (1, 1), (1, 2), (2, 0), (0, 4), (0, 5), (1, 3),
+    (0, 1), (1, 0), (0, 2), (0, 3), (1, 1), (1, 2), (2, 0), (0, 4), (0, 5), (1, 3),
     (2, 1), (1, 4), (1, 5), (3, 0), (2, 2), (3, 1), (2, 3), (3, 2), (2, 4), (2, 5), (3, 3),
     (3, 4), (3, 5),
 )
 
 
-def exchange(tables, params, states, peers, own_blocks, rooms):
-    tiles = states.shape[0] // ROWS
+def exchange(tables, own, own_row, ahead, peers, own_blocks, rooms):
+    tiles = own.shape[0] + 1
     planes = ROWS
     depths = peers // 2
     per = own_blocks // planes
@@ -421,16 +504,15 @@
         ),
         in_specs=[
             pl.BlockSpec(memory_space=pltpu.SMEM),
-            pl.BlockSpec(memory_space=pltpu.VMEM),
-            pl.BlockSpec(memory_space=pltpu.VMEM),
+            pl.BlockSpec(memory_space=pl.ANY),
+            pl.BlockSpec(memory_space=pl.ANY),
+            pl.BlockSpec(memory_space=pl.ANY),
         ],
         out_specs=(
             pl.BlockSpec(memory_space=pl.ANY),
             pl.BlockSpec(memory_space=pl.ANY),
         ),
         scratch_shapes=[
-            pltpu.VMEM((tiles, planes - 1, per, ROWS, LANES), f32),
-            pltpu.VMEM((planes - 1, per, LANES), f32),
             *buffers(own_blocks),
             *buffers(depths - 1, Z_STRIDE),
             *buffers(depths * Z_STRIDE),
@@ -440,13 +522,14 @@
             pltpu.SemaphoreType.DMA((tiles + 1, 3, planes)),
             pltpu.SemaphoreType.DMA((tiles + 1, 3, planes)),
             pltpu.SemaphoreType.DMA((tiles + 1,)),
+            pltpu.SemaphoreType.DMA((tiles + 1,)),
         ],
         compiler_params=pltpu.CompilerParams(
             collective_id=1 + TIERS.index(rooms),
             has_side_effects=True,
             vmem_limit_bytes=VMEM_LIMIT,
         ),
-    )(tables, params, states)
+    )(tables, own, own_row, ahead)
 
 
 def place_kernel(tiles, blocks, got, got_row, perm, out):
@@ -503,6 +586,10 @@
     capacity = 2 * local_blocks // devices
     partitions = jnp.arange(devices, dtype=jnp.int32)
     onehot = (block_part[:, None] == partitions[None, :]).astype(jnp.int32)
+    if counts_all is None:
+        counts_all = lax.all_gather(
+            jnp.sum(onehot, axis=0, dtype=jnp.int32), ("group", "peer")
+        )
     before = (partitions < d).astype(jnp.int32)
     earlier = jnp.sum(counts_all * before[:, None], axis=0, dtype=jnp.int32)
     rank_in = jnp.sum(
@@ -528,26 +615,19 @@
 def on_device(devices, peers, states, block_part, tile_perm, *gate_params):
     own_blocks = block_part.shape[0]
     width = states.shape[0]
-    partitions = jnp.arange(LANES, dtype=jnp.int32)
-    counts = jnp.sum(
-        (block_part[:, None] == partitions[None, :]).astype(jnp.int32), axis=0, dtype=jnp.int32
+    if (devices, peers) != (4 * ROWS, ROWS) or width % ROWS != 1:
+        return general(None, devices, states, block_part, tile_perm, *gate_params)
+    tables, tier, counts, own, own_row, ahead = opening(
+        block_part.reshape(1, own_blocks), [p.reshape(1, -1) for p in gate_params],
+        states, devices, peers,
     )
-    if (devices, peers) != (4 * ROWS, ROWS) or width % ROWS != 1:
-        gathered = lax.all_gather(counts[:devices], ("group", "peer"))
-        return general(gathered, devices, states, block_part, tile_perm, *gate_params)
-    gathered = gather_counts(counts.reshape(1, 1, LANES), devices, peers)
-    tables, tier = make_tables(
-        gathered, block_part.reshape(1, own_blocks), devices, peers, own_blocks
-    )
-    padded = jnp.stack([jnp.pad(p, (1, 0)) for p in gate_params])
-    params = jnp.broadcast_to(padded[:, :, None], padded.shape + (LANES,))
 
     def fast(rooms):
-        got, got_row = exchange(tables, params, states, peers, own_blocks, rooms)
+        got, got_row = exchange(tables, own, own_row, ahead, peers, own_blocks, rooms)
         return place(got, got_row, tile_perm, width, own_blocks)
 
     def slow():
-        matrix = gathered[:, 0, :devices]
+        matrix = counts[:, 0, :devices]
         return general(matrix, devices, states, block_part, tile_perm, *gate_params)
 
     choices = [functools.partial(fast, rooms) for rooms in TIERS] + [slow]

time: 201 us -> 187 us (0.930)
  Pallas kernels: 196 us -> 186 us
  local copies, waits for them, and re-layouts: 2.99 us -> 0 us
    pallas_call x1, Pallas kernels: 175 us -> 156 us  [exchange(): pl.pallas_call(functools.partial(exchange_kernel, peers, own_blocks, tile...]
    pallas_call x2 -> x1, Pallas kernels: 12.5 us -> 21.5 us  [opening(): pl.pallas_call(functools.partial(opening_kernel, devices, peers, own_bloc...]
    another operation x4 -> x0, local copies, waits for them, and re-layouts: 2.24 us -> none  [on_device(): padded = jnp.stack([jnp.pad(p, (1, 0)) for p in gate_params])]
where the time goes in v2:
time: 187 us; the launch traced here: 186 us
  Pallas kernels  186 us (99%)
    pallas_call x1, Pallas kernels, exchange(): pl.pallas_call(functools.partial(exchange_kernel, peers, own_blocks, tile...  156 us
    pallas_call x1, Pallas kernels, opening(): pl.pallas_call(functools.partial(opening_kernel, devices, peers, own_bloc...  21.5 us
    pallas_call x1, Pallas kernels, place(): pl.pallas_call(functools.partial(place_kernel, tiles, step), grid=(own_bl...  8.35 us

profile of v2, /device:TPU:9, one launch (start us, length us, event | category | flops | bytes accessed | tf_op | source)
XLA Modules:
  0.0 186.3 jit_solution(13374524171690065553)
XLA Ops:
  0.0 21.5 %shard_map.86 = (s32[16,128]{1,0:T(8,128)}, s32[1]{0:T(128)}, s32[32,1,128]{2,1,0:T(1,128)}, f32[4,8,32,8,128]{4,3,2,1,0:T(8,128)}, f32[8,32,128]{2,1,0:T(8,128)}, /*index=5*/f32[256,8,128]{2,1,0:T(8,128)}) custom-call(s32[1,256]{1,0:T(1,128)} %bitcast.62, f32[1,40]{1,0:T(1,128)} %bitcast.65, f32[1,40]{1,0:T(1,128)} %bitcast.66, f32[1,40]{1,0:T(1,128)} %bitcast.69, ...), custom_call_target="tpu_custom_call" | custom-call | tf_op jit(solution)/shard_map/pallas_call | solution.py:317
  22.2 164.2 %conditional.1 = (f32[41,32768]{1,0:T(8,128)}) conditional(s32[]{:T(128)} %bitcast.22, (s32[16,128]{1,0:T(8,128)}, f32[4,8,32,8,128]{4,3,2,1,0:T(8,128)}, f32[8,32,128]{2,1,0:T(8,128)}, f32[256,8,128]{2,1,0:T(8,128)}, s32[256,128]{1,0:T(8,128)}) %tuple.17, (s32[16,128]{1,0:T(8,128)}, f32[4,8,32,8,128]{4,3,2,1,0:T(8,128)}, ...), branch_computations={%region_0.0_spmd, %region_1.0_spmd, %region_2.0_spmd, %region_3.11... | conditional | flops 24065960 | bytes 187456160 | solution.py:634
  22.2 155.8 %branch_0_fun.2 = (f32[5,256,8,128]{3,2,1,0:T(8,128)}, f32[256,128]{1,0:T(8,128)}) custom-call(s32[16,128]{1,0:T(8,128)} %get-tuple-element.56.tables, f32[4,8,32,8,128]{4,3,2,1,0:T(8,128)} %get-tuple-element.58.own, f32[8,32,128]{2,1,0:T(8,128)} %get-tuple-element.60.own_row, f32[256,8,128]{2,1,0:T(8,128)} %get-tuple-element.61.ahead), custom_call_target="tpu_custom_call" | custom-call | tf_op jit(solution)/shard_map/cond/branch_0_fun/pallas_call | solution.py:499
  178.0 8.4 %branch_0_fun.3 = f32[41,32768]{1,0:T(8,128)} custom-call(f32[5,256,8,128]{3,2,1,0:T(8,128)} %get-tuple-element.62.got, f32[256,128]{1,0:T(8,128)} %get-tuple-element.63.got_row, s32[256,128]{1,0:T(8,128)} %get-tuple-element.64.perm), custom_call_target="tpu_custom_call" | custom-call | tf_op jit(solution)/shard_map/cond/branch_0_fun/pallas_call | solution.py:555

commit v3 on v2

--- a/solution.py
+++ b/solution.py
@@ -169,17 +169,35 @@
     tier_ref[0] = tier
 
 
-def opening_kernel(
-    devices, peers, own_blocks, tiles,
-    part_ref, half_ref, steep_ref, rate_ref, cond_ref, rev_ref, states_ref,
-    tab_ref, tier_ref, counts_out, own_out, row_out, first_out,
-    states, params, own, own_row, landed, tally, counts,
-    load_sem, count_send, count_recv, send_sem, recv_sem, out_sem,
-):
+def chunk_list(tiles):
+    half = ROWS // 2
+    chunks = [(0, 0, half), (0, half, half)]
+    chunks += [(t, 0, ROWS) for t in range(1, tiles - 1)]
+    return chunks + [(tiles - 1, 0, half), (tiles - 1, half, half), (tiles, 0, 1)]
+
+
+def chunk_shape(chunk, *lead):
+    return lead + ((chunk[2], LANES) if chunk[2] > 1 else (LANES,))
+
+
+def opening_kernel(devices, peers, own_blocks, chunks, *refs):
+    (
+        part_ref, half_ref, steep_ref, rate_ref, cond_ref, rev_ref, states_ref,
+        tab_ref, tier_ref, counts_out, first_out,
+    ) = refs[:11]
+    refs = refs[11:]
+    later = len(chunks) - 1
+    own_outs, refs = refs[:later], refs[later:]
+    owns, refs = refs[: later + 1], refs[later + 1 :]
+    (
+        states, params, landed, tally, counts,
+        load_sem, count_send, count_recv, send_sem, recv_sem, out_sem,
+    ) = refs
     d = my_index(peers)
     plane = plane_of(d, peers)
     depth = depth_of(d, peers)
     planes = ROWS
+    tiles = chunks[-1][0]
     per = own_blocks // planes
     step = per // PIECES
     width = step * planes * LANES
@@ -229,24 +247,28 @@
             new = steady + (vals - steady) * damping
             return new, cond * new * (v - rev)
 
+        def keep(tile, value):
+            for c, (t, lo, rows) in enumerate(chunks[:-1]):
+                if t == tile:
+                    if c == 0 and u == 0:
+                        landed[plane * per + i] = value[lo : lo + rows]
+                    else:
+                        owns[c][u, i] = value[lo : lo + rows]
+
         total = jnp.zeros((ROWS, LANES), jnp.float32)
         for t in range(1, tiles):
             new, term = gates(states[t * ROWS : (t + 1) * ROWS, cols], t * ROWS, ROWS)
-            own[t - 1, u, i] = new
+            keep(t, new)
             total = total + term
         last = tiles * ROWS
         new_row, term_row = gates(states[last : last + 1, cols], last, 1)
-        own_row[u, pl.ds(i, 1), :] = new_row
+        owns[-1][u, pl.ds(i, 1), :] = new_row
         new, term = gates(top, 0, ROWS)
         total = total + term
         current = jnp.sum(total, axis=0, keepdims=True) + term_row
         moved = voltage - time_step * current
         first = lax.broadcasted_iota(jnp.int32, (ROWS, LANES), 0) == 0
-        value = jnp.where(first, jnp.broadcast_to(moved, (ROWS, LANES)), new)
-        if u == 0:
-            landed[plane * per + i] = value
-        else:
-            own[tiles - 1, u, i] = value
+        keep(0, jnp.where(first, jnp.broadcast_to(moved, (ROWS, LANES)), new))
 
     def advance_loop(i, _):
         for u in range(planes):
@@ -273,7 +295,7 @@
         for m in (6, 7, 4, 5, 1, 3, 2):
             to = plane ^ m
             copy = pltpu.make_async_remote_copy(
-                src_ref=own.at[tiles - 1, m, pl.ds(q * step, step)],
+                src_ref=owns[0].at[m, pl.ds(q * step, step)],
                 dst_ref=landed.at[pl.ds(plane * per + q * step, step)],
                 send_sem=send_sem.at[q, m], recv_sem=recv_sem.at[q, m],
                 device_id=(to // 2, depth * 2 + to % 2), device_id_type=MESH_ID,
@@ -281,16 +303,12 @@
             copy.start()
             sends.append(copy)
         some = pl.ds(q * step, step)
-        copy = pltpu.make_async_copy(
-            own.at[pl.ds(0, tiles - 1), :, some], own_out.at[:, :, some], out_sem.at[q, 0]
-        )
-        copy.start()
-        outs.append(copy)
-        copy = pltpu.make_async_copy(
-            own_row.at[:, some], row_out.at[:, some], out_sem.at[q, 1]
-        )
-        copy.start()
-        outs.append(copy)
+        for c in range(later):
+            copy = pltpu.make_async_copy(
+                owns[c + 1].at[:, some], own_outs[c].at[:, some], out_sem.at[q, c]
+            )
+            copy.start()
+            outs.append(copy)
     for copy in count_copies:
         copy.wait_recv()
     counts_out[...] = counts[...]
@@ -312,28 +330,28 @@
     planes = ROWS
     per = own_blocks // planes
     f32 = jnp.float32
+    chunks = chunk_list(tiles)
     vmem = pl.BlockSpec(memory_space=pltpu.VMEM)
+    smem = pl.BlockSpec(memory_space=pltpu.SMEM)
     anywhere = pl.BlockSpec(memory_space=pl.ANY)
+    owns = [chunk_shape(c, planes, per) for c in chunks]
+    first = chunk_shape(chunks[0], own_blocks)
     return pl.pallas_call(
-        functools.partial(opening_kernel, devices, peers, own_blocks, tiles),
+        functools.partial(opening_kernel, devices, peers, own_blocks, chunks),
         out_shape=(
             jax.ShapeDtypeStruct((2 * ROWS, LANES), jnp.int32),
             jax.ShapeDtypeStruct((1,), jnp.int32),
             jax.ShapeDtypeStruct((devices, 1, LANES), jnp.int32),
-            jax.ShapeDtypeStruct((tiles - 1, planes, per, ROWS, LANES), f32),
-            jax.ShapeDtypeStruct((planes, per, LANES), f32),
-            jax.ShapeDtypeStruct((own_blocks, ROWS, LANES), f32),
+            jax.ShapeDtypeStruct(first, f32),
+            *[jax.ShapeDtypeStruct(o, f32) for o in owns[1:]],
         ),
         in_specs=[vmem] * 6 + [anywhere],
-        out_specs=(
-            vmem, pl.BlockSpec(memory_space=pltpu.SMEM), vmem, anywhere, anywhere, anywhere,
-        ),
+        out_specs=(vmem, smem, vmem, *[anywhere] * len(chunks)),
         scratch_shapes=[
+            *[pltpu.VMEM(o, f32) for o in owns],
             pltpu.VMEM(states.shape, f32),
             pltpu.VMEM((5, (tiles + 1) * ROWS, LANES), f32),
-            pltpu.VMEM((tiles, planes, per, ROWS, LANES), f32),
-            pltpu.VMEM((planes, per, LANES), f32),
-            pltpu.VMEM((own_blocks, ROWS, LANES), f32),
+            pltpu.VMEM(first, f32),
             pltpu.VMEM((1, LANES), jnp.int32),
             pltpu.VMEM((devices, 1, LANES), jnp.int32),
             pltpu.SemaphoreType.DMA((PIECES,)),
@@ -341,7 +359,7 @@
             pltpu.SemaphoreType.DMA((devices,)),
             pltpu.SemaphoreType.DMA((PIECES, planes)),
             pltpu.SemaphoreType.DMA((PIECES, planes)),
-            pltpu.SemaphoreType.DMA((PIECES + 1, 2)),
+            pltpu.SemaphoreType.DMA((PIECES + 1, len(chunks))),
         ],
         compiler_params=pltpu.CompilerParams(
             collective_id=0, has_side_effects=True, vmem_limit_bytes=VMEM_LIMIT
@@ -349,24 +367,23 @@
     )(part, *gate_params, states)
 
 
-def exchange_kernel(peers, own_blocks, tiles, rooms, tables, own, own_row, ahead, out, out_row, *refs):
+def exchange_kernel(peers, own_blocks, chunks, rooms, tables, perm, ahead, *refs):
     d = my_index(peers)
     plane = plane_of(d, peers)
     depth = depth_of(d, peers)
     planes = ROWS
     depths = peers // 2
     per = own_blocks // planes
-    chunks = tiles + 1
-    unroll = 8
-    at = 0
+    number = len(chunks)
+    owns, refs = refs[: number - 1], refs[number - 1 :]
+    out, refs = refs[0], refs[1:]
     groups = []
-    for _ in range(6):
-        groups.append(refs[at : at + chunks])
-        at += chunks
-    landed1, packed2, landed2, packed3, landed3, ready = groups
-    send_sem, recv_sem, out_sem, in_sem = refs[at:]
-    room2 = (None, Z_NEAR, rooms[0], rooms[0])
-    room3 = rooms[1]
+    for _ in range(5):
+        groups.append(refs[:number])
+        refs = refs[number:]
+    landed1, packed2, landed2, packed3, landed3 = groups
+    placed, row_ready, send_sem, recv_sem, out_sem, in_sem = refs
+    room2, room3 = rooms
     wide = planes * P_TABLE // LANES
 
     def device(to_plane, to_depth):
@@ -377,39 +394,25 @@
     partners += [device(plane, depth ^ m) for m in range(1, depths)]
     for to in partners:
         pl.semaphore_signal(barrier, inc=1, device_id=to, device_id_type=MESH_ID)
-
     loads = [pltpu.make_async_copy(ahead, landed1[0], in_sem.at[0])]
-    for c in range(1, chunks):
-        source = own.at[c - 1, 0] if c < tiles else own_row.at[0]
+    for c in range(1, number):
         loads.append(
             pltpu.make_async_copy(
-                source, landed1[c].at[pl.ds(plane * per, per)], in_sem.at[c]
+                owns[c - 1].at[0], landed1[c].at[pl.ds(plane * per, per)], in_sem.at[c]
             )
         )
     for copy in loads:
         copy.start()
     pl.semaphore_wait(barrier, len(partners))
 
-    copies = {}
-
-    def send(c, phase, m, src, dst, to):
-        copy = pltpu.make_async_remote_copy(
-            src_ref=src,
-            dst_ref=dst,
-            send_sem=send_sem.at[c, phase, m],
-            recv_sem=recv_sem.at[c, phase, m],
-            device_id=to,
-            device_id_type=MESH_ID,
-        )
-        copy.start()
-        copies[(c, phase, m)] = copy
-
     def gather(c, count, table_row, table_col, src, put, first):
+        unroll = 8
+
         def body(i, _):
             for u in range(unroll):
                 k = i * unroll + u
                 where = tables[table_row, table_col + k]
-                if c < tiles:
+                if chunks[c][2] > 1:
                     put[first + k] = src[where]
                 else:
                     put[pl.ds(first + k, 1), :] = src[pl.ds(where, 1), :]
@@ -417,41 +420,62 @@
 
         lax.fori_loop(0, count // unroll, body, 0)
 
+    def message(c, phase, m):
+        if phase == 0:
+            src = owns[c - 1].at[m]
+            dst = landed1[c].at[pl.ds(plane * per, per)]
+        elif phase == 1:
+            room = room2 if not isinstance(m, int) or m > 1 else Z_NEAR
+            src = packed2[c].at[m - 1, pl.ds(0, room)]
+            dst = landed2[c].at[pl.ds(depth * Z_STRIDE, room)]
+        else:
+            src = packed3[c].at[m - 1, pl.ds(0, room3)]
+            dst = landed3[c].at[pl.ds(plane * P_STRIDE, room3)]
+        to = device(plane, depth ^ m) if phase == 1 else device(plane ^ m, depth)
+        return pltpu.make_async_remote_copy(
+            src_ref=src, dst_ref=dst,
+            send_sem=send_sem.at[c, phase, m], recv_sem=recv_sem.at[c, phase, m],
+            device_id=to, device_id_type=MESH_ID,
+        )
+
     def phase1(c):
-        source = own.at[c - 1] if c < tiles else own_row
-        for m in (6, 7, 4, 5, 1, 3, 2):
-            send(
-                c, 0, m, source.at[m], landed1[c].at[pl.ds(plane * per, per)],
-                device(plane ^ m, depth),
-            )
+        def body(i, _):
+            message(c, 0, planes - 1 - i).start()
+            return 0
+
+        lax.fori_loop(0, planes - 1, body, 0)
 
     def phase2(c):
         loads[c].wait()
         for m in range(1, planes if c else 1):
-            copies[(c, 0, m)].wait_recv()
-        for m in (2, 3, 1):
-            gather(c, room2[m], depth ^ m, 0, landed1[c], packed2[c].at[m - 1], 0)
-            send(
-                c, 1, m, packed2[c].at[m - 1, pl.ds(0, room2[m])],
-                landed2[c].at[pl.ds(depth * Z_STRIDE, room2[m])],
-                device(plane, depth ^ m),
-            )
+            message(c, 0, m).wait_recv()
+
+        def body(i, _):
+            m = i + 2
+            gather(c, room2, depth ^ m, 0, landed1[c], packed2[c].at[m - 1], 0)
+            message(c, 1, m).start()
+            return 0
+
+        lax.fori_loop(0, depths - 2, body, 0)
+        gather(c, Z_NEAR, depth ^ 1, 0, landed1[c], packed2[c].at[0], 0)
+        message(c, 1, 1).start()
         gather(c, Z_NEAR, depth, 0, landed1[c], landed2[c], depth * Z_STRIDE)
 
     def phase3(c):
         for m in range(1, depths):
-            copies[(c, 1, m)].wait_recv()
-        for m in (6, 7, 4, 5, 1, 3, 2):
+            message(c, 1, m).wait_recv()
+
+        def body(i, _):
+            m = planes - 1 - i
             to = plane ^ m
             gather(
                 c, room3, depths + to // 2, (to % 2) * P_TABLE,
                 landed2[c], packed3[c].at[m - 1], 0,
             )
-            send(
-                c, 2, m, packed3[c].at[m - 1, pl.ds(0, room3)],
-                landed3[c].at[pl.ds(plane * P_STRIDE, room3)],
-                device(to, depth),
-            )
+            message(c, 2, m).start()
+            return 0
+
+        lax.fori_loop(0, planes - 1, body, 0)
         gather(
             c, room3, depths + plane // 2, (plane % 2) * P_TABLE,
             landed2[c], landed3[c], plane * P_STRIDE,
@@ -459,110 +483,103 @@
 
     outs = []
 
+    def turn(values, order):
+        return jnp.take_along_axis(values, order, axis=1, mode="promise_in_bounds")
+
     def finish(c):
         for m in range(1, planes):
-            copies[(c, 2, m)].wait_recv()
-        for t in range(own_blocks // LANES):
-            gather(c, LANES, depths + wide + t, 0, landed3[c], ready[c], t * LANES)
-        copy = pltpu.make_async_copy(
-            ready[c], out.at[c] if c < tiles else out_row, out_sem.at[c]
-        )
-        copy.start()
-        outs.append(copy)
+            message(c, 2, m).wait_recv()
+        tile, low, rows = chunks[c]
+        base = tile * ROWS + low
+        first = depths + wide
+
+        def body(i, _):
+            for u in range(ROWS):
+                b = i * ROWS + u
+                where = tables[first + b // LANES, b % LANES]
+                cols = pl.ds(pl.multiple_of(b * LANES, LANES), LANES)
+                order = jnp.broadcast_to(perm[pl.ds(b, 1), :], (rows, LANES))
+                placed[base : base + rows, cols] = turn(landed3[c][where], order)
+            return 0
+
+        def row_body(i, _):
+            eight = pl.ds(pl.multiple_of(i * ROWS, ROWS), ROWS)
+            for u in range(ROWS):
+                b = i * ROWS + u
+                where = tables[first + b // LANES, b % LANES]
+                row_ready[u : u + 1, :] = landed3[c][pl.ds(where, 1), :]
+            turned = turn(row_ready[...], perm[eight, :])
+            for u in range(ROWS):
+                cols = pl.ds(pl.multiple_of((i * ROWS + u) * LANES, LANES), LANES)
+                placed[base : base + 1, cols] = turned[u : u + 1, :]
+            return 0
+
+        lax.fori_loop(0, own_blocks // ROWS, body if rows > 1 else row_body, 0)
+        if low + rows == ROWS or rows == 1:
+            some = pl.ds(tile * ROWS, low + rows)
+            copy = pltpu.make_async_copy(placed.at[some], out.at[some], out_sem.at[tile])
+            copy.start()
+            outs.append(copy)
 
     for phase, c in EVENTS:
         (phase1, phase2, phase3, finish)[phase](c)
     for copy in outs:
         copy.wait()
-    for copy in copies.values():
-        copy.wait_send()
+    for c in range(number):
+        for m in range(1, planes):
+            if c:
+                message(c, 0, m).wait_send()
+            message(c, 2, m).wait_send()
+        for m in range(1, depths):
+            message(c, 1, m).wait_send()
 
 
 EVENTS = (
-    (0, 1), (1, 0), (0, 2), (0, 3), (1, 1), (1, 2), (2, 0), (0, 4), (0, 5), (1, 3),
-    (2, 1), (1, 4), (1, 5), (3, 0), (2, 2), (3, 1), (2, 3), (3, 2), (2, 4), (2, 5), (3, 3),
-    (3, 4), (3, 5),
+    (0, 1), (0, 2), (1, 0), (0, 3), (1, 1), (2, 0), (1, 2), (0, 4), (2, 1), (1, 3),
+    (0, 5), (0, 6), (0, 7), (3, 0), (1, 4), (2, 2), (3, 1), (1, 5), (1, 6), (1, 7),
+    (2, 3), (3, 2), (3, 3), (2, 4), (2, 5), (3, 4), (3, 5), (2, 6), (2, 7), (3, 6), (3, 7),
 )
 
 
-def exchange(tables, own, own_row, ahead, peers, own_blocks, rooms):
-    tiles = own.shape[0] + 1
+def exchange(tables, perm, ahead, owns, width, peers, own_blocks, rooms):
     planes = ROWS
     depths = peers // 2
-    per = own_blocks // planes
+    tiles = width // ROWS
+    chunks = chunk_list(tiles)
     f32 = jnp.float32
 
     def buffers(*lead):
-        kinds = [pltpu.VMEM(lead + (ROWS, LANES), f32) for _ in range(tiles)]
-        return kinds + [pltpu.VMEM(lead + (LANES,), f32)]
-
+        return [pltpu.VMEM(chunk_shape(c, *lead), f32) for c in chunks]
+
+    anywhere = pl.BlockSpec(memory_space=pl.ANY)
     return pl.pallas_call(
-        functools.partial(exchange_kernel, peers, own_blocks, tiles, rooms),
-        out_shape=(
-            jax.ShapeDtypeStruct((tiles, own_blocks, ROWS, LANES), f32),
-            jax.ShapeDtypeStruct((own_blocks, LANES), f32),
-        ),
+        functools.partial(exchange_kernel, peers, own_blocks, chunks, rooms),
+        out_shape=jax.ShapeDtypeStruct((width, own_blocks * LANES), f32),
         in_specs=[
             pl.BlockSpec(memory_space=pltpu.SMEM),
-            pl.BlockSpec(memory_space=pl.ANY),
-            pl.BlockSpec(memory_space=pl.ANY),
-            pl.BlockSpec(memory_space=pl.ANY),
+            pl.BlockSpec(memory_space=pltpu.VMEM),
+            *[anywhere] * len(chunks),
         ],
-        out_specs=(
-            pl.BlockSpec(memory_space=pl.ANY),
-            pl.BlockSpec(memory_space=pl.ANY),
-        ),
+        out_specs=anywhere,
         scratch_shapes=[
             *buffers(own_blocks),
             *buffers(depths - 1, Z_STRIDE),
             *buffers(depths * Z_STRIDE),
             *buffers(planes - 1, P_STRIDE),
             *buffers(planes * P_STRIDE),
-            *buffers(own_blocks),
-            pltpu.SemaphoreType.DMA((tiles + 1, 3, planes)),
-            pltpu.SemaphoreType.DMA((tiles + 1, 3, planes)),
+            pltpu.VMEM((width, own_blocks * LANES), f32),
+            pltpu.VMEM((ROWS, LANES), f32),
+            pltpu.SemaphoreType.DMA((len(chunks), 3, planes)),
+            pltpu.SemaphoreType.DMA((len(chunks), 3, planes)),
             pltpu.SemaphoreType.DMA((tiles + 1,)),
-            pltpu.SemaphoreType.DMA((tiles + 1,)),
+            pltpu.SemaphoreType.DMA((len(chunks),)),
         ],
         compiler_params=pltpu.CompilerParams(
             collective_id=1 + TIERS.index(rooms),
             has_side_effects=True,
             vmem_limit_bytes=VMEM_LIMIT,
         ),
-    )(tables, own, own_row, ahead)
-
-
-def place_kernel(tiles, blocks, got, got_row, perm, out):
-    for group in range(blocks // ROWS):
-        rows = slice(group * ROWS, (group + 1) * ROWS)
-        turned = jnp.take_along_axis(
-            got_row[rows, :], perm[rows, :], axis=1, mode="promise_in_bounds"
-        )
-        for u in range(ROWS):
-            b = group * ROWS + u
-            cols = slice(b * LANES, (b + 1) * LANES)
-            where = jnp.broadcast_to(perm[b : b + 1, :], (ROWS, LANES))
-            for t in range(tiles):
-                out[t * ROWS : (t + 1) * ROWS, cols] = jnp.take_along_axis(
-                    got[t, b], where, axis=1, mode="promise_in_bounds"
-                )
-            out[tiles * ROWS : tiles * ROWS + 1, cols] = turned[u : u + 1, :]
-
-
-def place(got, got_row, perm, width, own_blocks):
-    tiles = got.shape[0]
-    step = 32
-    return pl.pallas_call(
-        functools.partial(place_kernel, tiles, step),
-        grid=(own_blocks // step,),
-        out_shape=jax.ShapeDtypeStruct((width, own_blocks * LANES), jnp.float32),
-        in_specs=[
-            pl.BlockSpec((tiles, step, ROWS, LANES), lambda i: (0, i, 0, 0)),
-            pl.BlockSpec((step, LANES), lambda i: (i, 0)),
-            pl.BlockSpec((step, LANES), lambda i: (i, 0)),
-        ],
-        out_specs=pl.BlockSpec((width, step * LANES), lambda i: (0, i)),
-    )(got, got_row, perm)
+    )(tables, perm, ahead, *owns)
 
 
 def advance(state_rows, half_volt, steepness, gate_rate, conductance, reversal):
@@ -617,14 +634,13 @@
     width = states.shape[0]
     if (devices, peers) != (4 * ROWS, ROWS) or width % ROWS != 1:
         return general(None, devices, states, block_part, tile_perm, *gate_params)
-    tables, tier, counts, own, own_row, ahead = opening(
+    tables, tier, counts, ahead, *owns = opening(
         block_part.reshape(1, own_blocks), [p.reshape(1, -1) for p in gate_params],
         states, devices, peers,
     )
 
     def fast(rooms):
-        got, got_row = exchange(tables, own, own_row, ahead, peers, own_blocks, rooms)
-        return place(got, got_row, tile_perm, width, own_blocks)
+        return exchange(tables, tile_perm, ahead, owns, width, peers, own_blocks, rooms)
 
     def slow():
         matrix = counts[:, 0, :devices]

time: 187 us -> 197 us (1.053)
  local copies, waits for them, and re-layouts: 0 us -> 5.89 us
  Pallas kernels: 186 us -> 189 us
    pallas_call x2 -> x1, Pallas kernels: 164 us -> 173 us  [exchange(): pl.pallas_call(functools.partial(exchange_kernel, peers, own_blocks, chun...]
    unnamed x0 -> x1, local copies, waits for them, and re-layouts: none -> 5.89 us
    pallas_call x1, Pallas kernels: 21.5 us -> 16 us  [opening(): pl.pallas_call(functools.partial(opening_kernel, devices, peers, own_bloc...]
where the time goes in v3:
time: 197 us; the launch traced here: 196 us
  Pallas kernels  189 us (96%)
  local copies, waits for them, and re-layouts  5.89 us (3%)
    pallas_call x1, Pallas kernels, exchange(): pl.pallas_call(functools.partial(exchange_kernel, peers, own_blocks, chun...  173 us
    pallas_call x1, Pallas kernels, opening(): pl.pallas_call(functools.partial(opening_kernel, devices, peers, own_bloc...  16 us
    unnamed x1, local copies, waits for them, and re-layouts  5.89 us

profile of v3, /device:TPU:9, one launch (start us, length us, event | category | flops | bytes accessed | tf_op | source)
XLA Modules:
  0.0 195.8 jit_solution(4417559488539016641)
XLA Ops:
  0.0 16.0 %shard_map.86 = (s32[16,128]{1,0:T(8,128)}, s32[1]{0:T(128)}, s32[32,1,128]{2,1,0:T(1,128)}, f32[256,4,128]{2,1,0:T(4,128)}, f32[8,32,4,128]{3,2,1,0:T(4,128)}, ...) custom-call(s32[1,256]{1,0:T(1,128)} %bitcast.62, ...), custom_call_target="tpu_custom_call" | custom-call | tf_op jit(solution)/shard_map/pallas_call | solution.py:339
  16.7 173.2 %conditional.1 = (f32[41,32768]{1,0:T(8,128)}) conditional(s32[]{:T(128)} %bitcast.22, (s32[16,128]{1,0:T(8,128)}, s32[256,128]{1,0:T(8,128)}, f32[256,4,128]{2,1,0:T(4,128)}, f32[8,32,4,128]{3,2,1,0:T(4,128)}, f32[8,32,8,128]{3,2,1,0:T(8,128)}, /*index=5*/f32[8,32,8,128]{3,2,1,0:T(8,128)}, ...), branch_computations={%region_0.0_spmd, %region_1.0_spmd, %region_2.0_spmd, %region_3.11... | conditional | flops 24065960 | bytes 187456160 | solution.py:650
  16.7 173.0 %branch_0_fun.1 = f32[41,32768]{1,0:T(8,128)} custom-call(s32[16,128]{1,0:T(8,128)} %get-tuple-element.86.tables, s32[256,128]{1,0:T(8,128)} %get-tuple-element.88.perm, f32[256,4,128]{2,1,0:T(4,128)} %get-tuple-element.90.ahead, f32[8,32,4,128]{3,2,1,0:T(4,128)} %get-tuple-element.91.refs_0_, f32[8,32,8,128]{3,2,1,0:T(8,128)} %get-tuple-element.92.refs_1_, ...), custom_call_target="tpu_custom_call" | custom-call | tf_op jit(solution)/shard_map/cond/branch_0_fun/pallas_call | solution.py:555
  189.9 5.9 %copy.65 = f32[41,32768]{1,0:T(8,128)} copy(f32[41,32768]{1,0:T(8,128)} %get-tuple-element.165) | data formatting | bytes 10747904

commit v4 on v3

--- a/solution.py
+++ b/solution.py
@@ -17,7 +17,7 @@
 P_STRIDE = 48
 P_TABLE = 64
 PIECES = 4
-TIERS = ((72, 40), (80, 40), (88, 48))
+TIERS = ((70, 40), (74, 40), (88, 48))
 
 
 def my_index(peers):
@@ -171,8 +171,8 @@
 
 def chunk_list(tiles):
     half = ROWS // 2
-    chunks = [(0, 0, half), (0, half, half)]
-    chunks += [(t, 0, ROWS) for t in range(1, tiles - 1)]
+    chunks = [(1, 0, half), (1, half, half), (0, 0, ROWS)]
+    chunks += [(t, 0, ROWS) for t in range(2, tiles - 1)]
     return chunks + [(tiles - 1, 0, half), (tiles - 1, half, half), (tiles, 0, 1)]
 
 
@@ -190,7 +190,7 @@
     own_outs, refs = refs[:later], refs[later:]
     owns, refs = refs[: later + 1], refs[later + 1 :]
     (
-        states, params, landed, tally, counts,
+        states, params, landed, sums, tally, counts,
         load_sem, count_send, count_recv, send_sem, recv_sem, out_sem,
     ) = refs
     d = my_index(peers)
@@ -202,14 +202,17 @@
     step = per // PIECES
     width = step * planes * LANES
 
+    lead = 2 * ROWS
+    height = states_ref.shape[0]
     loads = []
-    for q in range(PIECES):
-        cols = pl.ds(q * width, width)
-        copy = pltpu.make_async_copy(
-            states_ref.at[:, cols], states.at[:, cols], load_sem.at[q]
-        )
-        copy.start()
-        loads.append(copy)
+    for part, (low, high) in enumerate(((0, lead), (lead, height))):
+        for q in range(PIECES):
+            some = (pl.ds(low, high - low), pl.ds(q * width, width))
+            copy = pltpu.make_async_copy(
+                states_ref.at[some], states.at[some], load_sem.at[part, q]
+            )
+            copy.start()
+            loads.append(copy)
 
     barrier = pltpu.get_barrier_semaphore()
     for k in range(1, devices):
@@ -230,45 +233,58 @@
             column = jnp.sum(jnp.where(chosen, ref[...], 0.0), axis=1, keepdims=True)
             params[k, base : base + ROWS, :] = jnp.broadcast_to(column, (ROWS, LANES))
 
+    def columns(i, u):
+        return pl.ds(pl.multiple_of((i * planes + u) * LANES, LANES), LANES)
+
+    def spread_of(cols):
+        spread = jnp.broadcast_to(states[0:1, cols], (ROWS, LANES))
+        return spread, -(1.0 + jax.nn.sigmoid(spread))
+
+    def gates(spread, slow, cols, base, count):
+        half, steep, rate, cond, rev = (
+            params[k, base : base + count, :] for k in range(5)
+        )
+        vals = states[base : base + count, cols]
+        v = spread[0:count]
+        steady = jax.nn.sigmoid((v - half) * steep)
+        damping = jnp.exp(rate * slow[0:count])
+        new = steady + (vals - steady) * damping
+        return new, cond * new * (v - rev)
+
+    def keep(tile, value, i, u):
+        for c, (t, lo, rows) in enumerate(chunks[:-1]):
+            if t == tile:
+                if c == 0 and u == 0:
+                    landed[plane * per + i] = value[lo : lo + rows]
+                else:
+                    owns[c][u, i] = value[lo : lo + rows]
+
+    def early_loop(i, _):
+        for u in range(planes):
+            cols = columns(i, u)
+            spread, slow = spread_of(cols)
+            new, term = gates(spread, slow, cols, ROWS, ROWS)
+            keep(1, new, i, u)
+            sums[i * planes + u] = term
+        return 0
+
     def advance_block(i, u):
-        cols = pl.ds(pl.multiple_of((i * planes + u) * LANES, LANES), LANES)
-        top = states[0:ROWS, cols]
-        voltage = top[0:1, :]
-        spread = jnp.broadcast_to(voltage, (ROWS, LANES))
-        slow = -(1.0 + jax.nn.sigmoid(spread))
-
-        def gates(vals, base, count):
-            half, steep, rate, cond, rev = (
-                params[k, base : base + count, :] for k in range(5)
-            )
-            v = spread[0:count]
-            steady = jax.nn.sigmoid((v - half) * steep)
-            damping = jnp.exp(rate * slow[0:count])
-            new = steady + (vals - steady) * damping
-            return new, cond * new * (v - rev)
-
-        def keep(tile, value):
-            for c, (t, lo, rows) in enumerate(chunks[:-1]):
-                if t == tile:
-                    if c == 0 and u == 0:
-                        landed[plane * per + i] = value[lo : lo + rows]
-                    else:
-                        owns[c][u, i] = value[lo : lo + rows]
-
-        total = jnp.zeros((ROWS, LANES), jnp.float32)
-        for t in range(1, tiles):
-            new, term = gates(states[t * ROWS : (t + 1) * ROWS, cols], t * ROWS, ROWS)
-            keep(t, new)
+        cols = columns(i, u)
+        spread, slow = spread_of(cols)
+        total = sums[i * planes + u]
+        for t in range(2, tiles):
+            new, term = gates(spread, slow, cols, t * ROWS, ROWS)
+            keep(t, new, i, u)
             total = total + term
         last = tiles * ROWS
-        new_row, term_row = gates(states[last : last + 1, cols], last, 1)
+        new_row, term_row = gates(spread, slow, cols, last, 1)
         owns[-1][u, pl.ds(i, 1), :] = new_row
-        new, term = gates(top, 0, ROWS)
+        new, term = gates(spread, slow, cols, 0, ROWS)
         total = total + term
         current = jnp.sum(total, axis=0, keepdims=True) + term_row
-        moved = voltage - time_step * current
+        moved = states[0:1, cols] - time_step * current
         first = lax.broadcasted_iota(jnp.int32, (ROWS, LANES), 0) == 0
-        keep(0, jnp.where(first, jnp.broadcast_to(moved, (ROWS, LANES)), new))
+        keep(0, jnp.where(first, jnp.broadcast_to(moved, (ROWS, LANES)), new), i, u)
 
     def advance_loop(i, _):
         for u in range(planes):
@@ -280,7 +296,7 @@
     count_copies = []
     for q in range(PIECES):
         loads[q].wait()
-        lax.fori_loop(q * step, (q + 1) * step, advance_loop, 0)
+        lax.fori_loop(q * step, (q + 1) * step, early_loop, 0)
         if q == 0:
             pl.semaphore_wait(barrier, devices - 1)
             for k in range(1, devices):
@@ -302,6 +318,9 @@
             )
             copy.start()
             sends.append(copy)
+    for q in range(PIECES):
+        loads[PIECES + q].wait()
+        lax.fori_loop(q * step, (q + 1) * step, advance_loop, 0)
         some = pl.ds(q * step, step)
         for c in range(later):
             copy = pltpu.make_async_copy(
@@ -352,9 +371,10 @@
             pltpu.VMEM(states.shape, f32),
             pltpu.VMEM((5, (tiles + 1) * ROWS, LANES), f32),
             pltpu.VMEM(first, f32),
+            pltpu.VMEM((own_blocks, ROWS, LANES), f32),
             pltpu.VMEM((1, LANES), jnp.int32),
             pltpu.VMEM((devices, 1, LANES), jnp.int32),
-            pltpu.SemaphoreType.DMA((PIECES,)),
+            pltpu.SemaphoreType.DMA((2, PIECES)),
             pltpu.SemaphoreType.DMA((devices,)),
             pltpu.SemaphoreType.DMA((devices,)),
             pltpu.SemaphoreType.DMA((PIECES, planes)),
@@ -367,7 +387,7 @@
     )(part, *gate_params, states)
 
 
-def exchange_kernel(peers, own_blocks, chunks, rooms, tables, perm, ahead, *refs):
+def exchange_kernel(peers, own_blocks, chunks, rooms, tables, ahead, *refs):
     d = my_index(peers)
     plane = plane_of(d, peers)
     depth = depth_of(d, peers)
@@ -376,14 +396,14 @@
     per = own_blocks // planes
     number = len(chunks)
     owns, refs = refs[: number - 1], refs[number - 1 :]
-    out, refs = refs[0], refs[1:]
+    out, out_row, refs = refs[0], refs[1], refs[2:]
     groups = []
     for _ in range(5):
         groups.append(refs[:number])
         refs = refs[number:]
     landed1, packed2, landed2, packed3, landed3 = groups
-    placed, row_ready, send_sem, recv_sem, out_sem, in_sem = refs
-    room2, room3 = rooms
+    ready, ready_row, send_sem, recv_sem, out_sem, in_sem = refs
+    near, room3 = Z_NEAR, rooms[1]
     wide = planes * P_TABLE // LANES
 
     def device(to_plane, to_depth):
@@ -425,7 +445,8 @@
             src = owns[c - 1].at[m]
             dst = landed1[c].at[pl.ds(plane * per, per)]
         elif phase == 1:
-            room = room2 if not isinstance(m, int) or m > 1 else Z_NEAR
+            room = near if m == 1 else rooms[0]
+            room = room if chunks[c][2] > 1 else -(-room // ROWS) * ROWS
             src = packed2[c].at[m - 1, pl.ds(0, room)]
             dst = landed2[c].at[pl.ds(depth * Z_STRIDE, room)]
         else:
@@ -445,25 +466,28 @@
 
         lax.fori_loop(0, planes - 1, body, 0)
 
-    def phase2(c):
+    waited = set()
+
+    def arrive(c, phase, m):
+        if (c, phase, m) not in waited:
+            waited.add((c, phase, m))
+            message(c, phase, m).wait_recv()
+
+    def phase2(c, gate):
         loads[c].wait()
         for m in range(1, planes if c else 1):
-            message(c, 0, m).wait_recv()
-
-        def body(i, _):
-            m = i + 2
-            gather(c, room2, depth ^ m, 0, landed1[c], packed2[c].at[m - 1], 0)
+            arrive(c, 0, m)
+        for m in (2, 3, 1):
+            if gate is not None:
+                arrive(gate, 1, m)
+            room = near if m == 1 else -(-rooms[0] // ROWS) * ROWS
+            gather(c, room, depth ^ m, 0, landed1[c], packed2[c].at[m - 1], 0)
             message(c, 1, m).start()
-            return 0
-
-        lax.fori_loop(0, depths - 2, body, 0)
-        gather(c, Z_NEAR, depth ^ 1, 0, landed1[c], packed2[c].at[0], 0)
-        message(c, 1, 1).start()
-        gather(c, Z_NEAR, depth, 0, landed1[c], landed2[c], depth * Z_STRIDE)
+        gather(c, near, depth, 0, landed1[c], landed2[c], depth * Z_STRIDE)
 
     def phase3(c):
         for m in range(1, depths):
-            message(c, 1, m).wait_recv()
+            arrive(c, 1, m)
 
         def body(i, _):
             m = planes - 1 - i
@@ -483,46 +507,34 @@
 
     outs = []
 
-    def turn(values, order):
-        return jnp.take_along_axis(values, order, axis=1, mode="promise_in_bounds")
-
     def finish(c):
         for m in range(1, planes):
-            message(c, 2, m).wait_recv()
+            arrive(c, 2, m)
         tile, low, rows = chunks[c]
-        base = tile * ROWS + low
         first = depths + wide
 
         def body(i, _):
             for u in range(ROWS):
                 b = i * ROWS + u
                 where = tables[first + b // LANES, b % LANES]
-                cols = pl.ds(pl.multiple_of(b * LANES, LANES), LANES)
-                order = jnp.broadcast_to(perm[pl.ds(b, 1), :], (rows, LANES))
-                placed[base : base + rows, cols] = turn(landed3[c][where], order)
+                if rows > 1:
+                    ready[tile, b, low : low + rows] = landed3[c][where]
+                else:
+                    ready_row[pl.ds(b, 1), :] = landed3[c][pl.ds(where, 1), :]
             return 0
 
-        def row_body(i, _):
-            eight = pl.ds(pl.multiple_of(i * ROWS, ROWS), ROWS)
-            for u in range(ROWS):
-                b = i * ROWS + u
-                where = tables[first + b // LANES, b % LANES]
-                row_ready[u : u + 1, :] = landed3[c][pl.ds(where, 1), :]
-            turned = turn(row_ready[...], perm[eight, :])
-            for u in range(ROWS):
-                cols = pl.ds(pl.multiple_of((i * ROWS + u) * LANES, LANES), LANES)
-                placed[base : base + 1, cols] = turned[u : u + 1, :]
-            return 0
-
-        lax.fori_loop(0, own_blocks // ROWS, body if rows > 1 else row_body, 0)
-        if low + rows == ROWS or rows == 1:
-            some = pl.ds(tile * ROWS, low + rows)
-            copy = pltpu.make_async_copy(placed.at[some], out.at[some], out_sem.at[tile])
-            copy.start()
-            outs.append(copy)
-
-    for phase, c in EVENTS:
-        (phase1, phase2, phase3, finish)[phase](c)
+        lax.fori_loop(0, own_blocks // ROWS, body, 0)
+        if rows == 1:
+            copy = pltpu.make_async_copy(ready_row, out_row, out_sem.at[tile])
+        elif low + rows == ROWS:
+            copy = pltpu.make_async_copy(ready.at[tile], out.at[tile], out_sem.at[tile])
+        else:
+            return
+        copy.start()
+        outs.append(copy)
+
+    for phase, *c in EVENTS:
+        (phase1, phase2, phase3, finish)[phase](*c)
     for copy in outs:
         copy.wait()
     for c in range(number):
@@ -535,13 +547,14 @@
 
 
 EVENTS = (
-    (0, 1), (0, 2), (1, 0), (0, 3), (1, 1), (2, 0), (1, 2), (0, 4), (2, 1), (1, 3),
-    (0, 5), (0, 6), (0, 7), (3, 0), (1, 4), (2, 2), (3, 1), (1, 5), (1, 6), (1, 7),
-    (2, 3), (3, 2), (3, 3), (2, 4), (2, 5), (3, 4), (3, 5), (2, 6), (2, 7), (3, 6), (3, 7),
+    (0, 1), (1, 0, None), (0, 2), (0, 3), (1, 1, 0), (2, 0), (1, 2, 1), (0, 4), (2, 1),
+    (1, 3, 2), (3, 0), (0, 5), (0, 6), (0, 7), (2, 2), (1, 4, 3), (3, 1), (2, 3), (3, 2),
+    (1, 5, 4), (2, 4), (1, 6, 5), (1, 7, None), (3, 3), (2, 5), (3, 4), (2, 6), (2, 7),
+    (3, 5), (3, 6), (3, 7),
 )
 
 
-def exchange(tables, perm, ahead, owns, width, peers, own_blocks, rooms):
+def exchange(tables, ahead, owns, width, peers, own_blocks, rooms):
     planes = ROWS
     depths = peers // 2
     tiles = width // ROWS
@@ -554,21 +567,20 @@
     anywhere = pl.BlockSpec(memory_space=pl.ANY)
     return pl.pallas_call(
         functools.partial(exchange_kernel, peers, own_blocks, chunks, rooms),
-        out_shape=jax.ShapeDtypeStruct((width, own_blocks * LANES), f32),
-        in_specs=[
-            pl.BlockSpec(memory_space=pltpu.SMEM),
-            pl.BlockSpec(memory_space=pltpu.VMEM),
-            *[anywhere] * len(chunks),
-        ],
-        out_specs=anywhere,
+        out_shape=(
+            jax.ShapeDtypeStruct((tiles, own_blocks, ROWS, LANES), f32),
+            jax.ShapeDtypeStruct((own_blocks, LANES), f32),
+        ),
+        in_specs=[pl.BlockSpec(memory_space=pltpu.SMEM), *[anywhere] * len(chunks)],
+        out_specs=(anywhere, anywhere),
         scratch_shapes=[
             *buffers(own_blocks),
             *buffers(depths - 1, Z_STRIDE),
             *buffers(depths * Z_STRIDE),
             *buffers(planes - 1, P_STRIDE),
             *buffers(planes * P_STRIDE),
-            pltpu.VMEM((width, own_blocks * LANES), f32),
-            pltpu.VMEM((ROWS, LANES), f32),
+            pltpu.VMEM((tiles, own_blocks, ROWS, LANES), f32),
+            pltpu.VMEM((own_blocks, LANES), f32),
             pltpu.SemaphoreType.DMA((len(chunks), 3, planes)),
             pltpu.SemaphoreType.DMA((len(chunks), 3, planes)),
             pltpu.SemaphoreType.DMA((tiles + 1,)),
@@ -579,7 +591,44 @@
             has_side_effects=True,
             vmem_limit_bytes=VMEM_LIMIT,
         ),
-    )(tables, perm, ahead, *owns)
+    )(tables, ahead, *owns)
+
+
+def place_kernel(tiles, blocks, got, got_row, perm, out):
+    def body(group, _):
+        rows = pl.ds(pl.multiple_of(group * ROWS, ROWS), ROWS)
+        orders = perm[rows, :]
+        turned = jnp.take_along_axis(
+            got_row[rows, :], orders, axis=1, mode="promise_in_bounds"
+        )
+        for u in range(ROWS):
+            b = group * ROWS + u
+            cols = pl.ds(pl.multiple_of(b * LANES, LANES), LANES)
+            where = jnp.broadcast_to(orders[u : u + 1, :], (ROWS, LANES))
+            for t in range(tiles):
+                out[t * ROWS : (t + 1) * ROWS, cols] = jnp.take_along_axis(
+                    got[t, b], where, axis=1, mode="promise_in_bounds"
+                )
+            out[tiles * ROWS : tiles * ROWS + 1, cols] = turned[u : u + 1, :]
+        return 0
+
+    lax.fori_loop(0, blocks // ROWS, body, 0, unroll=2)
+
+
+def place(got, got_row, perm, width, own_blocks):
+    tiles = got.shape[0]
+    step = 64
+    return pl.pallas_call(
+        functools.partial(place_kernel, tiles, step),
+        grid=(own_blocks // step,),
+        out_shape=jax.ShapeDtypeStruct((width, own_blocks * LANES), jnp.float32),
+        in_specs=[
+            pl.BlockSpec((tiles, step, ROWS, LANES), lambda i: (0, i, 0, 0)),
+            pl.BlockSpec((step, LANES), lambda i: (i, 0)),
+            pl.BlockSpec((step, LANES), lambda i: (i, 0)),
+        ],
+        out_specs=pl.BlockSpec((width, step * LANES), lambda i: (0, i)),
+    )(got, got_row, perm)
 
 
 def advance(state_rows, half_volt, steepness, gate_rate, conductance, reversal):
@@ -640,7 +689,8 @@
     )
 
     def fast(rooms):
-        return exchange(tables, tile_perm, ahead, owns, width, peers, own_blocks, rooms)
+        got, got_row = exchange(tables, ahead, owns, width, peers, own_blocks, rooms)
+        return place(got, got_row, tile_perm, width, own_blocks)
 
     def slow():
         matrix = counts[:, 0, :devices]

time: 197 us -> 175 us (0.89)
  Pallas kernels: 189 us -> 172 us
  local copies, waits for them, and re-layouts: 5.89 us -> 0 us
    pallas_call x1, Pallas kernels: 173 us -> 149 us  [exchange(): pl.pallas_call(functools.partial(exchange_kernel, peers, own_blocks, chun...]
    pallas_call x0 -> x1, Pallas kernels: none -> 7.13 us  [place(): pl.pallas_call(functools.partial(place_kernel, tiles, step), grid=(own_bl...]
    unnamed x1 -> x0, local copies, waits for them, and re-layouts: 5.89 us -> none
where the time goes in v4:
time: 175 us; the launch traced here: 173 us
  Pallas kernels  172 us (98%)
    pallas_call x1, Pallas kernels, exchange(): pl.pallas_call(functools.partial(exchange_kernel, peers, own_blocks, chun...  149 us
    pallas_call x1, Pallas kernels, opening(): pl.pallas_call(functools.partial(opening_kernel, devices, peers, own_bloc...  16.1 us
    pallas_call x1, Pallas kernels, place(): pl.pallas_call(functools.partial(place_kernel, tiles, step), grid=(own_bl...  7.13 us

profile of v4, /device:TPU:9, one launch (start us, length us, event | category | flops | bytes accessed | tf_op | source)
XLA Modules:
  0.0 172.5 jit_solution(2079272588470746744)
XLA Ops:
  0.0 16.1 %shard_map.86 = (s32[16,128]{1,0:T(8,128)}, s32[1]{0:T(128)}, s32[32,1,128]{2,1,0:T(1,128)}, f32[256,4,128]{2,1,0:T(4,128)}, f32[8,32,4,128]{3,2,1,0:T(4,128)}, ...) custom-call(s32[1,256]{1,0:T(1,128)} %bitcast.62, ...), custom_call_target="tpu_custom_call" | custom-call | tf_op jit(solution)/shard_map/pallas_call | solution.py:358
  16.8 155.8 %conditional.1 = (f32[41,32768]{1,0:T(8,128)}) conditional(s32[]{:T(128)} %bitcast.22, (s32[16,128]{1,0:T(8,128)}, f32[256,4,128]{2,1,0:T(4,128)}, f32[8,32,4,128]{3,2,1,0:T(4,128)}, f32[8,32,8,128]{3,2,1,0:T(8,128)}, f32[8,32,8,128]{3,2,1,0:T(8,128)}, /*index=5*/f32[8,32,8,128]{3,2,1,0:T(8,128)}, ...), branch_computations={%region_0.0_spmd, %region_1.0_spmd, %region_2.0_spmd, %region_3.11... | conditional | flops 24065960 | bytes 187456160 | solution.py:700
  16.8 148.6 %branch_0_fun.2 = (f32[5,256,8,128]{3,2,1,0:T(8,128)}, f32[256,128]{1,0:T(8,128)}) custom-call(s32[16,128]{1,0:T(8,128)} %get-tuple-element.86.tables, f32[256,4,128]{2,1,0:T(4,128)} %get-tuple-element.88.ahead, f32[8,32,4,128]{3,2,1,0:T(4,128)} %get-tuple-element.90.refs_0_, f32[8,32,8,128]{3,2,1,0:T(8,128)} %get-tuple-element.91.refs_1_, ...), custom_call_target="tpu_custom_call" | custom-call | tf_op jit(solution)/shard_map/cond/branch_0_fun/pallas_call | solution.py:568
  165.4 7.1 %branch_0_fun.3 = f32[41,32768]{1,0:T(8,128)} custom-call(f32[5,256,8,128]{3,2,1,0:T(8,128)} %get-tuple-element.97.got, f32[256,128]{1,0:T(8,128)} %get-tuple-element.98.got_row, s32[256,128]{1,0:T(8,128)} %get-tuple-element.99.perm), custom_call_target="tpu_custom_call" | custom-call | tf_op jit(solution)/shard_map/cond/branch_0_fun/pallas_call | solution.py:621
